TPU v7x, 32 devices: a whole 2x2x4 slice. The times are simulated.
32 devices in a mesh: wide: 16 (over z, y, x), narrow: 2 (over core).
Axes of the slice: x: 2, y: 2, z: 4, core: 2. Of those that a mesh axis runs over, the one named last changes fastest.
Arguments:
- node_latent: bfloat16 [4096, 512], P(('wide', 'narrow')), may hold values from -6 to 6
- edge_latent: bfloat16 [16384, 512], P(('wide', 'narrow')), may hold values from -6 to 6
- node_cotangent: bfloat16 [4096, 512], P(('wide', 'narrow')), may hold values from -6 to 6
- w_first: bfloat16 [1536, 512], replicated, may hold values from -2 to 2
- bias_first: bfloat16 [512], replicated, may hold values from -4 to 4
- w_second: bfloat16 [512, 512], replicated, may hold values from -2 to 2
- bias_second: bfloat16 [512], replicated, may hold values from -4 to 4
- norm_gain: bfloat16 [512], replicated, may hold values from 0.099609375 to 1.8984375
- send_map: int32 [32, 4, 64], P(('wide', 'narrow')), may hold values from -1 to 127, as said below
- edge_sender: int32 [16384], P(('wide', 'narrow')), may hold values from 0 to 383, as said below
- edge_receiver: int32 [16384], P(('wide', 'narrow')), may hold values from 0 to 127
Outputs:
- node_grad: bfloat16 [4096, 512], P(('wide', 'narrow'))
- edge_grad: bfloat16 [16384, 512], P(('wide', 'narrow'))
- first_update: float32 [1536, 512], P('wide')
- second_update: float32 [512, 512], P('wide')
Inputs may be any that keep to these rules, and one draw needn't show every extreme that they name: `send_map`: -1 marks an unused slot; in each row the used slots come first, at most 64, about a third of them on average; in every draw some partition uses all 64 slots toward a wide neighbour; partitions at narrow index 0 send nothing toward block 3 of a lower neighbour and those at the last narrow index nothing toward a higher one. `edge_sender`: a value below 128 is a local node; 128 + k * 64 + s names slot s of received block k, and only slots that the sending partition uses are named.
All inputs are finite; a program needn't handle non-finite values.
Results may differ from a plain program's by a relative error of at most 0.0085.
Values may be sent and summed in bfloat16 or wider, within the bound.
No kernel may reach another device: no remote copies, remote signals or barrier semaphores. Data moves between devices by JAX's collectives and lax.ppermute only.
A program may use at most 64 MiB of HBM per device.

v0:
```python
import math

import jax
import jax.numpy as jnp
from jax import lax
from jax.sharding import PartitionSpec as P


def shifted(value, axis, steps):
    count = lax.axis_size(axis)
    pairs = [(source, (source + steps) % count) for source in range(count)]
    return lax.ppermute(value, axis, pairs)


def shifted_2(block, axis, distance):
    devices = range(lax.axis_size(axis))
    route = [(i - distance, i) for i in devices if i - distance in devices]
    return lax.ppermute(block, axis, route)


def neighbours(blocks, direction):
    higher = shifted(blocks[0], "wide", direction)
    lower = shifted(blocks[1], "wide", -direction)
    up_side = shifted_2(blocks[2], "narrow", direction)
    down_side = shifted_2(blocks[3], "narrow", -direction)
    return jnp.stack([higher, lower, up_side, down_side], 0)


def norm_parts(second_pre):
    mean_value = jnp.mean(second_pre, -1, keepdims=True)
    centered = second_pre - mean_value
    variance = jnp.mean(centered * centered, -1, keepdims=True)
    inv_std = lax.rsqrt(variance + 1e-05)
    return (centered * inv_std, inv_std)


def clip_share(grad_share, grad_sq, weight_sq, fan_rows):
    unit_ratio = jnp.sqrt((grad_sq + 1e-06) / (weight_sq + 1e-06))
    mean_ratio = jnp.mean(unit_ratio)
    factor = jnp.minimum(
        1.0 / (mean_ratio * jnp.sqrt(weight_sq + 1e-06)), 1.0 / jnp.sqrt(grad_sq + 1e-06)
    )
    return grad_share * factor * math.sqrt(fan_rows)


def edge_contract(hot_table, values):
    return lax.dot_general(
        hot_table,
        values,
        (((0,), (0,)), ((), ())),
        precision=lax.Precision.HIGHEST,
        preferred_element_type=jnp.float32,
    )


def per_device(
    node_latent,
    edge_latent,
    node_cotangent,
    w_first,
    bias_first,
    w_second,
    bias_second,
    norm_gain,
    send_map,
    edge_sender,
    edge_receiver,
):
    node_count, feature_width = node_latent.shape
    halo_slots = send_map.shape[2]
    table_rows = node_count + 4 * halo_slots
    send_hot = (send_map[0][:, :, None] == jnp.arange(node_count, dtype=jnp.int32)).astype(
        jnp.bfloat16
    )
    outgoing = jnp.einsum(
        "khn,nd->khd", send_hot, node_latent, preferred_element_type=jnp.float32
    ).astype(jnp.bfloat16)
    received = neighbours(outgoing, 1)
    node_table = jnp.concatenate([node_latent, received.reshape(4 * halo_slots, feature_width)], 0)
    sender_hot = (edge_sender[:, None] == jnp.arange(table_rows, dtype=jnp.int32)).astype(
        jnp.bfloat16
    )
    receiver_hot = (edge_receiver[:, None] == jnp.arange(node_count, dtype=jnp.int32)).astype(
        jnp.bfloat16
    )
    sender_rows = jnp.dot(sender_hot, node_table, preferred_element_type=jnp.float32).astype(
        jnp.bfloat16
    )
    receiver_rows = jnp.dot(receiver_hot, node_latent, preferred_element_type=jnp.float32).astype(
        jnp.bfloat16
    )
    inputs = jnp.concatenate([edge_latent, sender_rows, receiver_rows], 1)
    preact = jnp.dot(inputs, w_first, preferred_element_type=jnp.float32) + bias_first.astype(
        jnp.float32
    )
    activation = jax.nn.silu(preact).astype(jnp.bfloat16)
    second_pre = jnp.dot(
        activation, w_second, preferred_element_type=jnp.float32
    ) + bias_second.astype(jnp.float32)
    normalized, inv_std = norm_parts(second_pre)
    upstream = jnp.dot(receiver_hot, node_cotangent, preferred_element_type=jnp.float32)
    scaled = upstream * norm_gain.astype(jnp.float32)
    norm_back = (
        inv_std
        * (
            scaled
            - jnp.mean(scaled, -1, keepdims=True)
            - normalized * jnp.mean(scaled * normalized, -1, keepdims=True)
        )
    ).astype(jnp.bfloat16)
    second_grad = lax.dot_general(
        activation, norm_back, (((0,), (0,)), ((), ())), preferred_element_type=jnp.float32
    )
    sigmoid_pre = jax.nn.sigmoid(preact)
    pre_back = (
        jnp.dot(norm_back, w_second.T, preferred_element_type=jnp.float32)
        * sigmoid_pre
        * (1.0 + preact * (1.0 - sigmoid_pre))
    ).astype(jnp.bfloat16)
    first_grad = lax.dot_general(
        inputs, pre_back, (((0,), (0,)), ((), ())), preferred_element_type=jnp.float32
    )
    input_back = jnp.dot(pre_back, w_first.T, preferred_element_type=jnp.float32)
    edge_grad = (upstream + input_back[:, :feature_width]).astype(jnp.bfloat16)
    table_grad = edge_contract(
        sender_hot.astype(jnp.float32), input_back[:, feature_width : 2 * feature_width]
    )
    receiver_grad = edge_contract(
        receiver_hot.astype(jnp.float32), input_back[:, 2 * feature_width :]
    )
    halo_grad = table_grad[node_count:].reshape(4, halo_slots, feature_width).astype(jnp.bfloat16)
    returned = neighbours(halo_grad, -1)
    back = jnp.einsum("khn,khd->nd", send_hot, returned, preferred_element_type=jnp.float32)
    node_grad = (
        node_cotangent.astype(jnp.float32) + table_grad[:node_count] + receiver_grad + back
    ).astype(jnp.bfloat16)
    wide_count = lax.axis_size("wide")
    first_rows = w_first.shape[0] // wide_count
    second_rows = w_second.shape[0] // wide_count
    first_weight_sq = jnp.sum(jnp.square(w_first.astype(jnp.float32)), 0)
    second_weight_sq = jnp.sum(jnp.square(w_second.astype(jnp.float32)), 0)
    first_total, second_total = lax.psum((first_grad, second_grad), ("wide", "narrow"))
    position = lax.axis_index("wide")
    first_share = lax.dynamic_slice_in_dim(first_total, position * first_rows, first_rows, 0)
    second_share = lax.dynamic_slice_in_dim(second_total, position * second_rows, second_rows, 0)
    first_grad_sq = jnp.sum(first_total * first_total, 0)
    second_grad_sq = jnp.sum(second_total * second_total, 0)
    first_update = clip_share(first_share, first_grad_sq, first_weight_sq, w_first.shape[0])
    second_update = clip_share(second_share, second_grad_sq, second_weight_sq, w_second.shape[0])
    return (node_grad, edge_grad, first_update, second_update)


def solution(mesh):
    return jax.shard_map(
        per_device,
        mesh=mesh,
        in_specs=(
            P(("wide", "narrow"), None),
            P(("wide", "narrow"), None),
            P(("wide", "narrow"), None),
            P(),
            P(),
            P(),
            P(),
            P(),
            P(("wide", "narrow"), None, None),
            P(("wide", "narrow")),
            P(("wide", "narrow")),
        ),
        out_specs=(
            P(("wide", "narrow"), None),
            P(("wide", "narrow"), None),
            P("wide", None),
            P("wide", None),
        ),
        check_vma=False,
    )
```

profile of v0, /device:TPU:0, one launch (start us, length us, event | category | flops | bytes accessed | tf_op | source)
XLA Modules:
  0.0 192.4 jit_solution(14532633733271048976)
XLA Ops:
  7.2 0.0 copy-start.4
  7.2 0.0 copy-start.1
  7.2 0.0 all-reduce.3.cloned.1.call-start
  7.2 1.3 convolution_convert_fusion.2
  8.6 1.3 collective-permute-start.3
  9.9 3.0 %collective-permute-start.2 = (bf16[64,512]{1,0:T(8,128)(2,1)S(1)}, bf16[64,512]{1,0:T(8,128)(2,1)S(1)}, u32[]{:S(2)}, u32[]{:S(2)}) collective-permute-start(bf16[64,512]{1,0:T(8,128)(2,1)S(1)} %get-tuple-element.18), channel_id=1, source_target_pairs={{0,1},{2,3},{4,5},{6,7},{8,9},{10,11},{12,13},{14,15},{16,17},{18,... | collective-permute-start | bytes 196616 | tf_op jit(solution)/shard_map/ppermute | solution.py:18
  12.9 7.0 %collective-permute-start.1 = (bf16[64,512]{1,0:T(8,128)(2,1)S(1)}, bf16[64,512]{1,0:T(8,128)(2,1)S(1)}, u32[]{:S(2)}, u32[]{:S(2)}) collective-permute-start(bf16[64,512]{1,0:T(8,128)(2,1)S(1)} %get-tuple-element.19), channel_id=1, source_target_pairs={{0,30},{2,0},{4,2},{6,4},{8,6},{10,8},{12,10},{14,12},{16,14},{18,... | collective-permute-start | bytes 196616 | tf_op jit(solution)/shard_map/ppermute | solution.py:12
  19.9 1.3 convolution_convert_fusion.1
  21.3 0.7 convert_element_type.56
  22.0 0.7 convert_element_type.55
  22.6 1.3 copy.15
  23.9 0.7 convert_element_type.53
  24.6 3.2 %collective-permute-done = bf16[64,512]{1,0:T(8,128)(2,1)S(1)} collective-permute-done((bf16[64,512]{1,0:T(8,128)(2,1)S(1)}, bf16[64,512]{1,0:T(8,128)(2,1)S(1)}, u32[]{:S(2)}, u32[]{:S(2)}) %collective-permute-start) | collective-permute-done | bytes 65568 | tf_op jit(solution)/shard_map/ppermute | solution.py:12
  27.9 0.6 convolution_convert_fusion
  28.5 0.0 copy-start.5
  28.5 1.0 convolution_add_fusion.1
  29.5 0.0 copy-done.5
  29.5 0.6 fusion.33
  30.2 0.2 multiply_reduce_fusion.5
  30.4 0.1 copy-done.6
  30.4 0.5 multiply_reduce_fusion.6
  31.0 0.3 multiply_convert_fusion
  31.3 0.7 fusion.1
  31.9 0.1 copy-done
  32.0 1.5 fusion.31
  33.5 2.7 %fusion.7 = f32[1536,512]{1,0:T(8,128)} fusion(bf16[512,512]{1,0:T(8,128)(2,1)S(1)} %fusion.1, bf16[512,512]{0,1:T(8,128)(2,1)S(1)} %convolution_convert_fusion.1, bf16[512,512]{0,1:T(8,128)(2,1)S(1)} %convolution_convert_fusion, bf16[512,512]{0,1:T(8,128)(2,1)S(1)} %copy.15), kind=kOutput, calls=%fused_computation.28 | convolution fusion | flops 810024960 | bytes 5242880 | tf_op jit(solution)/shard_map/dot_general | solution.py:120
  36.2 0.0 all-reduce.3.cloned.1.call-update
  36.2 0.2 multiply_reduce_fusion.2
  36.4 0.4 multiply_reduce_fusion
  36.8 2.6 %fusion.35 = f32[512,1536]{1,0:T(8,128)S(1)} fusion(bf16[512,512]{1,0:T(8,128)(2,1)} %copy-done.3, bf16[1536,512]{1,0:T(8,128)(2,1)} %param.14), kind=kOutput, calls=%fused_computation.74 | convolution fusion | flops 805306368 | bytes 5242880 | tf_op jit(solution)/shard_map/dot_general | solution.py:123
  39.3 1.0 slice.69
  40.4 1.8 fusion.34
  42.3 1.9 collective-permute-start.7
  44.2 1.3 collective-permute-start.6
  45.5 0.1 collective-permute-start.5
  45.5 5.6 %collective-permute-start.4 = (bf16[64,512]{1,0:T(8,128)(2,1)S(1)}, bf16[64,512]{1,0:T(8,128)(2,1)}, u32[]{:S(2)}, u32[]{:S(2)}) collective-permute-start(bf16[64,512]{1,0:T(8,128)(2,1)S(1)} %get-tuple-element.12), channel_id=1, source_target_pairs={{0,30},{2,0},{4,2},{6,4},{8,6},{10,8},{12,10},{14,12},{16,14},{18,... | collective-permute-start | bytes 196616 | tf_op jit(solution)/shard_map/ppermute | solution.py:12
  51.1 2.6 %copy.18 = f32[512,512]{0,1:T(8,128)} copy(f32[512,512]{1,0:T(8,128)} %slice.69) | data formatting | bytes 2097152
  53.7 2.6 %add_convert_fusion = bf16[512,512]{0,1:T(8,128)(2,1)} fusion(f32[512,512]{0,1:T(8,128)} %copy-done, f32[512,512]{0,1:T(8,128)} %copy.18), kind=kLoop, calls=%fused_computation.20 | loop fusion | flops 524288 | bytes 2621440 | tf_op jit(solution)/shard_map/convert_element_type | solution.py:124
  56.2 2.3 %convolution_add_fusion.2 = f32[128,512]{1,0:T(8,128)} fusion(f32[512,1536]{1,0:T(8,128)S(1)} %fusion.35, f32[384,512]{1,0:T(8,128)} %get-tuple-element.24, bf16[128,512]{1,0:T(8,128)(2,1)S(1)} %copy-done.6, s32[512]{0:T(512)S(1)} %copy-done.7), kind=kOutput, calls=%fused_computation.12 | convolution fusion | flops 402915328 | bytes 1705984 | tf_op jit(solution)/shard_map/dot_general | solution.py:47
  58.5 2.0 %copy.17 = bf16[512,512]{1,0:T(8,128)(2,1)} copy(bf16[512,512]{0,1:T(8,128)(2,1)} %add_convert_fusion) | data formatting | bytes 1048576
  60.6 2.0 %fusion.3 = bf16[128,512]{1,0:T(8,128)(2,1)} fusion(f32[128,512]{1,0:T(8,128)} %convolution_add_fusion.2, bf16[1,64,512]{2,1,0:T(8,128)(2,1)} %bitcast.14, bf16[1,64,512]{2,1,0:T(8,128)(2,1)} %bitcast.13, bf16[1,64,512]{2,1,0:T(8,128)(2,1)} %bitcast.12, bf16[1,64,512]{2,1,0:T(8,128)(2,1)} %bitcast.11, s32[4,64]{1,0:T(4,128)S(1)} %bitcast.43), kind=kOutput, calls=%fused_computation.14 | convolution fusion | flops 34111488 | bytes 656384 | tf_op jit(solution)/shard_map/khn,khd->nd/dot_general | solution.py:133
  62.6 115.6 %all-reduce.3.cloned.1.call-done = (f32[1536,512]{1,0:T(8,128)}, f32[512,512]{1,0:T(8,128)}) async-done(((f32[1536,512]{1,0:T(8,128)}, f32[512,512]{1,0:T(8,128)}), (f32[1536,512]{1,0:T(8,128)}, f32[512,512]{1,0:T(8,128)})) %all-reduce.3.cloned.1.call-update) | async-done | bytes 4194320 | tf_op jit(solution)/shard_map/psum | solution.py:142
  178.3 2.3 %multiply_reduce_fusion.1 = f32[512]{0:T(512)S(1)} fusion(f32[1536,512]{1,0:T(8,128)} %get-tuple-element.10), kind=kLoop, calls=%fused_computation.1 | loop fusion | flops 1572352 | bytes 3147776 | tf_op jit(solution)/shard_map/reduce_sum | solution.py:146
  180.5 0.6 sqrt_reduce_fusion.1
  181.8 0.1 multiply_reduce_fusion.3
  182.0 0.6 sqrt_reduce_fusion
  183.2 1.6 multiply_multiply_fusion
  184.9 0.6 multiply_multiply_fusion.1
  (30 shorter events, 0.2 us)
Async XLA Ops:
  7.2 20.7 %copy-start.4 = (bf16[128,512]{1,0:T(8,128)(2,1)S(1)}, bf16[128,512]{1,0:T(8,128)(2,1)}, u32[]{:S(2)}) copy-start(bf16[128,512]{1,0:T(8,128)(2,1)} %param.11) | copy-start | bytes 393220
  7.2 20.7 %copy-start.8 = (s32[512]{0:T(512)S(1)}, s32[512]{0:T(512)}, u32[]{:S(2)}) copy-start(s32[512]{0:T(512)} %param.20) | copy-start | bytes 6148
  7.2 21.3 %copy-start.1 = (bf16[1536,512]{1,0:T(8,128)(2,1)S(1)}, bf16[1536,512]{1,0:T(8,128)(2,1)}, u32[]{:S(2)}) copy-start(bf16[1536,512]{1,0:T(8,128)(2,1)} %param.14) | copy-start | bytes 4718596
  7.2 171.1 %all-reduce.3.cloned.1.call-start = ((), (), s32[]{:S(2)}) async-start(), calls=%async_computation | async-start | bytes 8388608 | tf_op jit(solution)/shard_map/psum | solution.py:142
  8.6 16.0 %collective-permute-start.3 = (bf16[64,512]{1,0:T(8,128)(2,1)S(1)}, bf16[64,512]{1,0:T(8,128)(2,1)S(1)}, u32[]{:S(2)}, u32[]{:S(2)}) collective-permute-start(bf16[64,512]{1,0:T(8,128)(2,1)S(1)} %get-tuple-element.17), channel_id=1, source_target_pairs={{1,0},{3,2},{5,4},{7,6},{9,8},{11,10},{13,12},{15,14},{17,16},{19,... | collective-permute-start | bytes 196616 | tf_op jit(solution)/shard_map/ppermute | solution.py:18
  9.9 14.7 %collective-permute-start.2 = (bf16[64,512]{1,0:T(8,128)(2,1)S(1)}, bf16[64,512]{1,0:T(8,128)(2,1)S(1)}, u32[]{:S(2)}, u32[]{:S(2)}) collective-permute-start(bf16[64,512]{1,0:T(8,128)(2,1)S(1)} %get-tuple-element.18), channel_id=1, source_target_pairs={{0,1},{2,3},{4,5},{6,7},{8,9},{10,11},{12,13},{14,15},{16,17},{18,... | collective-permute-start | bytes 196616 | tf_op jit(solution)/shard_map/ppermute | solution.py:18
  12.9 11.7 %collective-permute-start.1 = (bf16[64,512]{1,0:T(8,128)(2,1)S(1)}, bf16[64,512]{1,0:T(8,128)(2,1)S(1)}, u32[]{:S(2)}, u32[]{:S(2)}) collective-permute-start(bf16[64,512]{1,0:T(8,128)(2,1)S(1)} %get-tuple-element.19), channel_id=1, source_target_pairs={{0,30},{2,0},{4,2},{6,4},{8,6},{10,8},{12,10},{14,12},{16,14},{18,... | collective-permute-start | bytes 196616 | tf_op jit(solution)/shard_map/ppermute | solution.py:12
  19.9 7.9 %collective-permute-start = (bf16[64,512]{1,0:T(8,128)(2,1)S(1)}, bf16[64,512]{1,0:T(8,128)(2,1)S(1)}, u32[]{:S(2)}, u32[]{:S(2)}) collective-permute-start(bf16[64,512]{1,0:T(8,128)(2,1)S(1)} %get-tuple-element.16), channel_id=1, source_target_pairs={{0,2},{2,4},{4,6},{6,8},{8,10},{10,12},{12,14},{14,16},{16,18},{18... | collective-permute-start | bytes 196616 | tf_op jit(solution)/shard_map/ppermute | solution.py:12
  28.5 1.0 copy-start.5
  29.5 0.9 copy-start.6
  29.5 0.9 copy-start.7
  30.9 1.1 copy-start
  32.0 1.5 copy-start.3
  42.3 18.3 %collective-permute-start.7 = (bf16[64,512]{1,0:T(8,128)(2,1)S(1)}, bf16[64,512]{1,0:T(8,128)(2,1)}, u32[]{:S(2)}, u32[]{:S(2)}) collective-permute-start(bf16[64,512]{1,0:T(8,128)(2,1)S(1)} %get-tuple-element.13), channel_id=1, source_target_pairs={{0,1},{2,3},{4,5},{6,7},{8,9},{10,11},{12,13},{14,15},{16,17},{18,... | collective-permute-start | bytes 196616 | tf_op jit(solution)/shard_map/ppermute | solution.py:18
  44.2 16.4 %collective-permute-start.6 = (bf16[64,512]{1,0:T(8,128)(2,1)S(1)}, bf16[64,512]{1,0:T(8,128)(2,1)}, u32[]{:S(2)}, u32[]{:S(2)}) collective-permute-start(bf16[64,512]{1,0:T(8,128)(2,1)S(1)} %get-tuple-element.14), channel_id=1, source_target_pairs={{1,0},{3,2},{5,4},{7,6},{9,8},{11,10},{13,12},{15,14},{17,16},{19,... | collective-permute-start | bytes 196616 | tf_op jit(solution)/shard_map/ppermute | solution.py:18
  45.5 15.1 %collective-permute-start.5 = (bf16[64,512]{1,0:T(8,128)(2,1)S(1)}, bf16[64,512]{1,0:T(8,128)(2,1)}, u32[]{:S(2)}, u32[]{:S(2)}) collective-permute-start(bf16[64,512]{1,0:T(8,128)(2,1)S(1)} %get-tuple-element.15), channel_id=1, source_target_pairs={{0,2},{2,4},{4,6},{6,8},{8,10},{10,12},{12,14},{14,16},{16,18},{18... | collective-permute-start | bytes 196616 | tf_op jit(solution)/shard_map/ppermute | solution.py:12
  45.5 15.0 %collective-permute-start.4 = (bf16[64,512]{1,0:T(8,128)(2,1)S(1)}, bf16[64,512]{1,0:T(8,128)(2,1)}, u32[]{:S(2)}, u32[]{:S(2)}) collective-permute-start(bf16[64,512]{1,0:T(8,128)(2,1)S(1)} %get-tuple-element.12), channel_id=1, source_target_pairs={{0,30},{2,0},{4,2},{6,4},{8,6},{10,8},{12,10},{14,12},{16,14},{18,... | collective-permute-start | bytes 196616 | tf_op jit(solution)/shard_map/ppermute | solution.py:12
  53.7 6.9 %copy-start.9 = (s32[1,4,64]{2,1,0:T(4,128)S(1)}, s32[1,4,64]{2,1,0:T(4,128)}, u32[]{:S(2)}) copy-start(s32[1,4,64]{2,1,0:T(4,128)} %param.19) | copy-start | bytes 3076
  178.3 3.5 %copy-start.2 = (f32[512,512]{1,0:T(8,128)S(1)}, f32[512,512]{1,0:T(8,128)}, u32[]{:S(2)}) copy-start(f32[512,512]{1,0:T(8,128)} %get-tuple-element.11) | copy-start | bytes 3145732
Sparse Core Ops, SparseCore 0:
  36.3 141.9 all-reduce.2
where the time goes:
time: 193 us; the launch traced here: 192 us
  waiting for transfers between devices  119 us (62%)
  starting transfers between devices  20.2 us (10%)
  matrix products  18.9 us (10%)
  between operations  15.6 us (8%)
  other arithmetic  11.6 us (6%)
  local copies, waits for them, and re-layouts  7.15 us (4%)
    psum x1, waiting for transfers between devices, per_device(): lax.psum((first_grad, second_grad), ('wide', 'narrow'))  116 us
    ppermute x4, starting transfers between devices, shifted(): return lax.ppermute(value, axis, pairs)  12.7 us
    ppermute x4, starting transfers between devices, shifted_2(): return lax.ppermute(block, axis, route)  7.52 us
    unnamed x23, local copies, waits for them, and re-layouts  6.07 us
    dot_general x2, matrix products, edge_contract(): lax.dot_general(hot_table, values, (((0,), (0,)), ((), ())), precision=la...  4.11 us
  transfers between devices with their start and end apart: 9, of which 2 were waited for; matrix products, arithmetic and copies ran while one was open for 12% of the time, Pallas kernels for 0%

commit v1 on v0

v1 whole, which is shorter than its diff:
```python
import math

import jax
import jax.numpy as jnp
from jax import lax
from jax.sharding import PartitionSpec as P

BF = jnp.bfloat16
F32 = jnp.float32


def halo_routes(axis, base, ring):
    count = lax.axis_size(axis)
    if count % 2:
        up = [(i, (i + 1) % count) for i in range(count) if ring or i + 1 < count]
        return [(up, base, base), ([(t, s) for s, t in up], base + 1, base + 1)]
    odd = lax.axis_index(axis) % 2
    near = [(i, i ^ 1) for i in range(count)]
    far = [(i, ((i + 1) ^ 1) - 1) for i in range(count)]
    far = [(s, t % count) for s, t in far if ring or 0 <= t < count]
    routes = [(near, base + odd, base + 1 - odd)]
    if far:
        routes.insert(0, (far, base + 1 - odd, base + odd))
    return routes


def norm_parts(second_pre):
    mean_value = jnp.mean(second_pre, -1, keepdims=True)
    centered = second_pre - mean_value
    variance = jnp.mean(centered * centered, -1, keepdims=True)
    inv_std = lax.rsqrt(variance + 1e-05)
    return (centered * inv_std, inv_std)


def clip_share(grad_share, grad_sq, weight_sq, fan_rows):
    unit_ratio = jnp.sqrt((grad_sq + 1e-06) / (weight_sq + 1e-06))
    mean_ratio = jnp.mean(unit_ratio)
    factor = jnp.minimum(
        1.0 / (mean_ratio * jnp.sqrt(weight_sq + 1e-06)), 1.0 / jnp.sqrt(grad_sq + 1e-06)
    )
    return grad_share * (factor * math.sqrt(fan_rows))


def contract(hot, values):
    high = values.astype(BF)
    low = (values - high.astype(F32)).astype(BF)
    dims = (((0,), (0,)), ((), ()))
    return lax.dot_general(hot, high, dims, preferred_element_type=F32) + lax.dot_general(
        hot, low, dims, preferred_element_type=F32
    )


def swap_pairs(size, mask):
    return [(i, i ^ mask) for i in range(size)]


def pick(value, axis, index):
    return lax.dynamic_index_in_dim(value, index, axis, keepdims=False)


def reduce_weights(first_grad, second_grad):
    wide, narrow = lax.axis_size("wide"), lax.axis_size("narrow")
    a, b = lax.axis_index("wide"), lax.axis_index("narrow")
    width = first_grad.shape[1]
    first_rows, second_rows = first_grad.shape[0] // wide, second_grad.shape[0] // wide
    rows = first_rows + second_rows
    value = jnp.concatenate(
        [
            first_grad.reshape(wide, first_rows, width),
            second_grad.reshape(wide, second_rows, width),
        ],
        1,
    )
    span, mask = width, narrow // 2
    while mask:
        span //= 2
        bit = (b // mask) % 2
        sent = lax.dynamic_slice_in_dim(value, (1 - bit) * span, span, 2).astype(BF)
        kept = lax.dynamic_slice_in_dim(value, bit * span, span, 2)
        value = kept + lax.ppermute(sent, "narrow", swap_pairs(narrow, mask)).astype(F32)
        mask //= 2
    bits = wide.bit_length() - 1
    low, high = a % 2, (a // 2) % 2
    flip = b % 2
    value = value.reshape(wide // 4, 2, 2, rows, span)
    both = ("wide", "narrow")

    def crossed(value, even_mask, odd_mask):
        pairs = []
        for i in range(wide):
            for j in range(narrow):
                pairs.append((i * narrow + j, (i ^ (odd_mask if j % 2 else even_mask)) * narrow + j))
        return lax.ppermute(value.astype(BF), both, pairs).astype(F32)

    sent = jnp.where(flip == 0, pick(value, 2, 1 - low), pick(value, 1, 1 - high))
    kept = jnp.where(flip == 0, pick(value, 2, low), pick(value, 1, high))
    value = kept + crossed(sent, 1, 2)
    left = jnp.where(flip == 0, high, low)
    value = pick(value, 1, left) + crossed(pick(value, 1, 1 - left), 2, 1)
    for position in range(2, bits - 1):
        value = value.reshape(value.shape[0] // 2, 2, rows, span)
        bit = (a >> position) % 2
        value = pick(value, 1, bit) + crossed(pick(value, 1, 1 - bit), 1 << position, 1 << position)
    top = wide // 2
    value = value.reshape(2, rows, span)
    value = value + crossed(value, top, top)
    mask = 1
    while mask < narrow:
        other = lax.ppermute(value, "narrow", swap_pairs(narrow, mask))
        bit = (b // mask) % 2
        value = jnp.where(
            bit == 0,
            jnp.concatenate([value, other], 2),
            jnp.concatenate([other, value], 2),
        )
        mask *= 2
    squares = value * value
    sums = jnp.stack([squares[:, :first_rows].sum((0, 1)), squares[:, first_rows:].sum((0, 1))], 0)
    for position in range(bits - 1):
        sums = sums + lax.ppermute(sums, "wide", swap_pairs(wide, 1 << position))
    share = pick(value, 0, a // top)
    return share[:first_rows], share[first_rows:], sums[0], sums[1]


def per_device(
    node_latent,
    edge_latent,
    node_cotangent,
    w_first,
    bias_first,
    w_second,
    bias_second,
    norm_gain,
    send_map,
    edge_sender,
    edge_receiver,
):
    node_count, feature_width = node_latent.shape
    halo_slots = send_map.shape[2]
    routes = [("wide", r) for r in halo_routes("wide", 0, True)]
    routes += [("narrow", r) for r in halo_routes("narrow", 2, False)]
    blocks = len(routes)
    table_rows = node_count + blocks * halo_slots
    sent_slots = jnp.stack([pick(send_map[0], 0, sent) for _, (_, sent, _) in routes], 0)
    send_hot = (sent_slots[:, :, None] == jnp.arange(node_count, dtype=jnp.int32)).astype(BF)
    outgoing = jnp.einsum(
        "khn,nd->khd", send_hot, node_latent, preferred_element_type=F32
    ).astype(BF)
    received = [
        lax.ppermute(outgoing[k], axis, pairs) for k, (axis, (pairs, _, _)) in enumerate(routes)
    ]
    node_table = jnp.concatenate([node_latent] + received, 0)
    block = (edge_sender - node_count) // halo_slots
    place = jnp.zeros_like(block)
    for k, (_, (_, _, taken)) in enumerate(routes):
        place = jnp.where(block == taken, k, place)
    sender = jnp.where(
        edge_sender < node_count, edge_sender, edge_sender + (place - block) * halo_slots
    )
    sender_hot = (sender[:, None] == jnp.arange(table_rows, dtype=jnp.int32)).astype(BF)
    receiver_hot = (edge_receiver[:, None] == jnp.arange(node_count, dtype=jnp.int32)).astype(BF)
    sender_rows = jnp.dot(sender_hot, node_table, preferred_element_type=F32).astype(BF)
    receiver_rows = jnp.dot(receiver_hot, node_latent, preferred_element_type=F32).astype(BF)
    inputs = jnp.concatenate([edge_latent, sender_rows, receiver_rows], 1)
    preact = jnp.dot(inputs, w_first, preferred_element_type=F32) + bias_first.astype(F32)
    activation = jax.nn.silu(preact).astype(BF)
    second_pre = jnp.dot(activation, w_second, preferred_element_type=F32) + bias_second.astype(F32)
    normalized, inv_std = norm_parts(second_pre)
    upstream = jnp.dot(receiver_hot, node_cotangent, preferred_element_type=F32)
    scaled = upstream * norm_gain.astype(F32)
    norm_back = (
        inv_std
        * (
            scaled
            - jnp.mean(scaled, -1, keepdims=True)
            - normalized * jnp.mean(scaled * normalized, -1, keepdims=True)
        )
    ).astype(BF)
    outer = (((0,), (0,)), ((), ()))
    second_grad = lax.dot_general(activation, norm_back, outer, preferred_element_type=F32)
    sigmoid_pre = jax.nn.sigmoid(preact)
    pre_back = (
        jnp.dot(norm_back, w_second.T, preferred_element_type=F32)
        * sigmoid_pre
        * (1.0 + preact * (1.0 - sigmoid_pre))
    ).astype(BF)
    first_grad = lax.dot_general(inputs, pre_back, outer, preferred_element_type=F32)
    input_back = jnp.dot(pre_back, w_first.T, preferred_element_type=F32)
    edge_grad = (upstream + input_back[:, :feature_width]).astype(BF)
    table_grad = contract(sender_hot, input_back[:, feature_width : 2 * feature_width])
    receiver_grad = contract(receiver_hot, input_back[:, 2 * feature_width :])
    halo_grad = table_grad[node_count:].reshape(blocks, halo_slots, feature_width).astype(BF)
    returned = jnp.stack(
        [
            lax.ppermute(halo_grad[k], axis, [(t, s) for s, t in pairs])
            for k, (axis, (pairs, _, _)) in enumerate(routes)
        ],
        0,
    )
    back = jnp.einsum("khn,khd->nd", send_hot, returned, preferred_element_type=F32)
    node_grad = (
        node_cotangent.astype(F32) + table_grad[:node_count] + receiver_grad + back
    ).astype(BF)
    first_weight_sq = jnp.sum(jnp.square(w_first.astype(F32)), 0)
    second_weight_sq = jnp.sum(jnp.square(w_second.astype(F32)), 0)
    first_share, second_share, first_grad_sq, second_grad_sq = reduce_weights(
        first_grad, second_grad
    )
    first_update = clip_share(first_share, first_grad_sq, first_weight_sq, w_first.shape[0])
    second_update = clip_share(second_share, second_grad_sq, second_weight_sq, w_second.shape[0])
    return (node_grad, edge_grad, first_update, second_update)


def solution(mesh):
    return jax.shard_map(
        per_device,
        mesh=mesh,
        in_specs=(
            P(("wide", "narrow"), None),
            P(("wide", "narrow"), None),
            P(("wide", "narrow"), None),
            P(),
            P(),
            P(),
            P(),
            P(),
            P(("wide", "narrow"), None, None),
            P(("wide", "narrow")),
            P(("wide", "narrow")),
        ),
        out_specs=(
            P(("wide", "narrow"), None),
            P(("wide", "narrow"), None),
            P("wide", None),
            P("wide", None),
        ),
        check_vma=False,
    )
```

time: 193 us -> 83.9 us (0.43)
  waiting for transfers between devices: 119 us -> 22.6 us
  between operations: 15.6 us -> 2.44 us
  other arithmetic: 11.6 us -> 19.5 us
  starting transfers between devices: 20.2 us -> 14 us
  matrix products: 18.9 us -> 13.7 us
  local copies, waits for them, and re-layouts: 7.15 us -> 10.8 us
    psum x1 -> x0, waiting for transfers between devices: 116 us -> none  [per_device(): lax.psum((first_grad, second_grad), ('wide', 'narrow'))]
    ppermute x8 -> x15, waiting for transfers between devices: 3.22 us -> 22.6 us  [the longest x4 15.8 us: crossed(): return lax.ppermute(value.astype(BF), both, pairs).astype(F32)]
    ppermute x8 -> x15, starting transfers between devices: 20.2 us -> 14 us  [the longest x3 7.03 us: per_device(): lax.ppermute(outgoing[k], axis, pairs)]
    dot_general x13 -> x15, matrix products: 18.9 us -> 13.7 us  [the longest x2 2.79 us: contract(): lax.dot_general(hot, low, dims, preferred_element_type=F32)]
    add x0 -> x8, other arithmetic: none -> 4.65 us  [the longest x1 2 us: reduce_weights(): kept + lax.ppermute(sent, 'narrow', swap_pairs(narrow, mask)).astype(F32)]
    unnamed x23 -> x39, local copies, waits for them, and re-layouts: 6.07 us -> 8.18 us
    mul x2 -> x4, other arithmetic: 2.27 us -> 4.04 us  [the longest x3 3.12 us: clip_share(): return grad_share * (factor * math.sqrt(fan_rows))]
    convert_element_type x4 -> x7, other arithmetic: 4.6 us -> 2.83 us  [the longest x1 2.53 us: per_device(): edge_grad = (upstream + input_back[:, :feature_width]).astype(BF)]
  transfers between devices with their start and end apart: 9 -> 15, of which waited for: 2 -> 8; matrix products, arithmetic and copies ran while one was open for 12% -> 28% of each run, Pallas kernels for 0% -> 0%
where the time goes in v1:
time: 83.9 us; the launch traced here: 83 us
  waiting for transfers between devices  22.6 us (27%)
  other arithmetic  19.5 us (23%)
  starting transfers between devices  14 us (17%)
  matrix products  13.7 us (16%)
  local copies, waits for them, and re-layouts  10.8 us (13%)
  between operations  2.44 us (3%)
    ppermute x4, waiting for transfers between devices, crossed(): return lax.ppermute(value.astype(BF), both, pairs).astype(F32)  15.8 us
    unnamed x39, local copies, waits for them, and re-layouts  8.18 us
    ppermute x3, starting transfers between devices, per_device(): lax.ppermute(outgoing[k], axis, pairs)  7.03 us
    ppermute x3, waiting for transfers between devices, reduce_weights(): sums = sums + lax.ppermute(sums, 'wide', swap_pairs(wide, 1 << position))  3.2 us
    mul x3, other arithmetic, clip_share(): return grad_share * (factor * math.sqrt(fan_rows))  3.12 us
    ppermute x1, waiting for transfers between devices, reduce_weights(): lax.ppermute(sent, 'narrow', swap_pairs(narrow, mask)).astype(F32)  2.79 us
    dot_general x2, matrix products, contract(): lax.dot_general(hot, low, dims, preferred_element_type=F32)  2.79 us
    ppermute x3, starting transfers between devices, reduce_weights(): sums = sums + lax.ppermute(sums, 'wide', swap_pairs(wide, 1 << position))  2.77 us
  transfers between devices with their start and end apart: 15, of which 8 were waited for; matrix products, arithmetic and copies ran while one was open for 28% of the time, Pallas kernels for 0%

profile of v1, /device:TPU:0, one launch (start us, length us, event | category | flops | bytes accessed | tf_op | source)
XLA Modules:
  0.0 83.0 jit_solution(5430705679073664321)
XLA Ops:
  0.7 0.8 fusion.46
  1.5 1.2 %convolution_convert_fusion.2 = bf16[3,64,512]{2,1,0:T(8,128)(2,1)S(1)} fusion(bf16[128,512]{1,0:T(8,128)(2,1)} %param.11, s32[3,64]{1,0:T(4,128)S(1)} %pad_add_fusion), kind=kOutput, calls=%fused_computation.18 | convolution fusion | flops 25288704 | bytes 328448 | tf_op jit(solution)/shard_map/khn,nd->khd/dot_general | solution.py:146
  2.7 7.0 %collective-permute-start = (bf16[64,512]{1,0:T(8,128)(2,1)S(1)}, bf16[64,512]{1,0:T(8,128)(2,1)S(1)}, u32[]{:S(2)}, u32[]{:S(2)}) collective-permute-start(bf16[64,512]{1,0:T(8,128)(2,1)S(1)} %get-tuple-element.19), channel_id=1, source_target_pairs={{0,30},{2,4},{4,2},{6,8},{8,6},{10,12},{12,10},{14,16},{16,14},{18... | collective-permute-start | bytes 196616 | tf_op jit(solution)/shard_map/ppermute | solution.py:150
  9.8 1.3 %convolution_convert_fusion.1 = bf16[512,512]{0,1:T(8,128)(2,1)S(1)} fusion(bf16[128,512]{1,0:T(8,128)(2,1)} %param.11, s32[512]{0:T(512)} %param.21), kind=kOutput, calls=%fused_computation.16 | convolution fusion | flops 67436544 | bytes 657408 | tf_op jit(solution)/shard_map/dot_general | solution.py:163
  11.1 0.7 compare_select_fusion
  11.8 1.3 %copy.18 = bf16[512,512]{0,1:T(8,128)(2,1)S(1)} copy(bf16[512,512]{1,0:T(8,128)(2,1)} %param.12) | data formatting | bytes 1048576 | tf_op args[1]
  13.2 0.9 %collective-permute-done.1 = bf16[64,512]{1,0:T(8,128)(2,1)S(1)} collective-permute-done((bf16[64,512]{1,0:T(8,128)(2,1)S(1)}, bf16[64,512]{1,0:T(8,128)(2,1)S(1)}, u32[]{:S(2)}, u32[]{:S(2)}) %collective-permute-start.1) | collective-permute-done | bytes 65568 | tf_op jit(solution)/shard_map/ppermute | solution.py:150
  14.0 0.6 convolution_convert_fusion
  14.7 1.0 %convolution_add_fusion.1 = f32[512,512]{1,0:T(8,128)S(1)} fusion(bf16[1536,512]{1,0:T(8,128)(2,1)S(1)} %copy-done.2, bf16[512,512]{0,1:T(8,128)(2,1)S(1)} %convolution_convert_fusion.1, bf16[512,512]{0,1:T(8,128)(2,1)S(1)} %convolution_convert_fusion, bf16[512,512]{0,1:T(8,128)(2,1)S(1)} %copy.18, f32[512]{0:T(512)S(1)} %convert_element_type.105), kind=kOutput, calls=%fused_computation.13 | convolution fusion | flops 810287104 | bytes 4196352 | tf_op jit(solution)/shard_map/dot_general | solution.py:165
  15.7 0.6 fusion.57
  17.4 0.7 fusion.5
  19.4 1.0 %fusion.14 = f32[1536,512]{1,0:T(8,128)S(1)} fusion(bf16[512,512]{1,0:T(8,128)(2,1)S(1)} %fusion.5, bf16[512,512]{0,1:T(8,128)(2,1)S(1)} %convolution_convert_fusion.1, bf16[512,512]{0,1:T(8,128)(2,1)S(1)} %convolution_convert_fusion, bf16[512,512]{0,1:T(8,128)(2,1)S(1)} %copy-done.12), kind=kOutput, calls=%fused_computation.46 | convolution fusion | flops 810024960 | bytes 5242880 | tf_op jit(solution)/shard_map/dot_general | solution.py:187
  20.5 1.5 %copy-done = f32[1536,512]{1,0:T(8,128)} copy-done((f32[1536,512]{1,0:T(8,128)}, f32[1536,512]{1,0:T(8,128)S(1)}, u32[]{:S(2)}) %copy-start) | copy-done | bytes 3145752
  22.0 2.8 %collective-permute-done.6 = bf16[16,128,256]{2,1,0:T(8,128)(2,1)} collective-permute-done((bf16[16,128,256]{2,1,0:T(8,128)(2,1)S(1)}, bf16[16,128,256]{2,1,0:T(8,128)(2,1)}, u32[]{:S(2)}, u32[]{:S(2)}) %collective-permute-start.6) | collective-permute-done | bytes 1048608 | tf_op jit(solution)/shard_map/ppermute | solution.py:80
  24.8 2.0 %fusion.3 = f32[16,128,256]{2,1,0:T(8,128)S(1)} fusion(s32[]{:T(128)S(6)} %select_n.134, f32[16,96,512]{2,1,0:T(8,128)} %bitcast.89, f32[16,32,512]{2,1,0:T(8,128)S(1)} %bitcast.91, bf16[16,128,256]{2,1,0:T(8,128)(2,1)} %collective-permute-done.6), kind=kLoop, calls=%fused_computation.8 | loop fusion | flops 1572864 | bytes 7340036 | tf_op jit(solution)/shard_map/add | solution.py:80
  26.9 1.4 %collective-permute-start.7 = (bf16[4,2,128,256]{3,2,0,1:T(8,128)(2,1)S(1)}, bf16[4,2,128,256]{3,2,0,1:T(8,128)(2,1)S(1)}, u32[]{:S(2)}, u32[]{:S(2)}) collective-permute-start(bf16[4,2,128,256]{3,2,0,1:T(8,128)(2,1)S(1)} %fusion.10), channel_id=1, source_target_pairs={{0,2},{1,5},{2,0},{3,7},{4,6},{5,1},{6,4},{7,3},{8,10},{9,13},{10,... | collective-permute-start | bytes 1572872 | tf_op jit(solution)/shard_map/ppermute | solution.py:93
  28.3 1.2 %multiply_reduce_fusion.1 = f32[512]{0:T(512)S(1)} fusion(bf16[512,512]{1,0:T(8,128)(2,1)} %param.16), kind=kLoop, calls=%fused_computation.32 | loop fusion | flops 785920 | bytes 526336 | tf_op jit(solution)/shard_map/reduce_sum | solution.py:205
  29.5 2.4 %multiply_reduce_fusion = f32[512]{0:T(512)} fusion(bf16[1536,512]{1,0:T(8,128)(2,1)} %param.14), kind=kLoop, calls=%fused_computation.4 | loop fusion | flops 2358784 | bytes 1574912 | tf_op jit(solution)/shard_map/reduce_sum | solution.py:204
  31.8 4.3 %collective-permute-done.7 = bf16[4,2,128,256]{3,2,0,1:T(8,128)(2,1)S(1)} collective-permute-done((bf16[4,2,128,256]{3,2,0,1:T(8,128)(2,1)S(1)}, bf16[4,2,128,256]{3,2,0,1:T(8,128)(2,1)S(1)}, u32[]{:S(2)}, u32[]{:S(2)}) %collective-permute-start.7) | collective-permute-done | bytes 524320 | tf_op jit(solution)/shard_map/ppermute | solution.py:93
  36.5 1.0 %fusion.59 = f32[512,1536]{1,0:T(8,128)S(1)} fusion(bf16[512,512]{1,0:T(8,128)(2,1)S(1)} %copy-done.7, bf16[1536,512]{1,0:T(8,128)(2,1)S(1)} %copy-done.3), kind=kOutput, calls=%fused_computation.134 | convolution fusion | flops 805306368 | bytes 5242880 | tf_op jit(solution)/shard_map/dot_general | solution.py:188
  37.5 5.3 %collective-permute-done.8 = bf16[4,128,256]{2,1,0:T(8,128)(2,1)S(1)} collective-permute-done((bf16[4,128,256]{2,1,0:T(8,128)(2,1)S(1)}, bf16[4,128,256]{2,1,0:T(8,128)(2,1)S(1)}, u32[]{:S(2)}, u32[]{:S(2)}) %collective-permute-start.8) | collective-permute-done | bytes 262176 | tf_op jit(solution)/shard_map/ppermute | solution.py:93
  43.0 0.5 fusion.13
  43.5 4.4 %collective-permute-done.9 = bf16[2,128,256]{2,1,0:T(8,128)(2,1)S(1)} collective-permute-done((bf16[2,128,256]{2,1,0:T(8,128)(2,1)S(1)}, bf16[2,128,256]{2,1,0:T(8,128)(2,1)S(1)}, u32[]{:S(2)}, u32[]{:S(2)}) %collective-permute-start.9) | collective-permute-done | bytes 131104 | tf_op jit(solution)/shard_map/ppermute | solution.py:93
  48.1 1.5 %fusion.58 = (bf16[320,512]{1,0:T(8,128)(2,1)}, f32[320,512]{1,0:T(8,128)}) fusion(f32[320,512]{1,0:T(8,128)S(1)} %fusion.13, f32[512,1536]{1,0:T(8,128)S(1)} %fusion.59, s32[512]{0:T(512)S(1)} %compare_select_fusion), kind=kOutput, calls=%fused_computation.133 | convolution fusion | flops 169312256 | bytes 2689024 | tf_op jit(solution)/shard_map/dot_general | solution.py:48
  49.5 1.1 %slice.89 = f32[512,512]{1,0:T(8,128)} slice(f32[512,1536]{1,0:T(8,128)S(1)} %fusion.59), slice={[0:512], [0:512]} | slice | bytes 2097152 | tf_op jit(solution)/shard_map/slice | solution.py:189
  50.6 2.5 %copy.25 = f32[512,512]{0,1:T(8,128)} copy(f32[512,512]{1,0:T(8,128)} %slice.89) | data formatting | bytes 2097152
  53.1 1.7 %collective-permute-done.10 = bf16[2,128,256]{2,1,0:T(8,128)(2,1)} collective-permute-done((bf16[2,128,256]{2,1,0:T(8,128)(2,1)S(1)}, bf16[2,128,256]{2,1,0:T(8,128)(2,1)}, u32[]{:S(2)}, u32[]{:S(2)}) %collective-permute-start.10) | collective-permute-done | bytes 131104 | tf_op jit(solution)/shard_map/ppermute | solution.py:93
  54.9 1.1 %convert_add_fusion = f32[2,128,256]{2,1,0:T(8,128)S(1)} fusion(bf16[2,128,256]{2,1,0:T(8,128)(2,1)} %collective-permute-done.10, bf16[2,128,256]{2,1,0:T(8,128)(2,1)S(1)} %collective-permute-done.9, f32[2,2,128,256]{3,2,1,0:T(8,128)} %bitcast.94, s32[]{:T(128)S(6)} %select_n.148), kind=kLoop, calls=%fused_computation.64 | loop fusion | flops 262144 | bytes 786436 | tf_op jit(solution)/shard_map/add | solution.py:106
  56.0 2.5 %add_convert_fusion = bf16[512,512]{0,1:T(8,128)(2,1)} fusion(f32[512,512]{0,1:T(8,128)} %copy-done.1, f32[512,512]{0,1:T(8,128)} %copy.25), kind=kLoop, calls=%fused_computation.33 | loop fusion | flops 524288 | bytes 2621440 | tf_op jit(solution)/shard_map/convert_element_type | solution.py:189
  58.9 0.9 %fusion.55 = (f32[2,128,512]{2,1,0:T(8,128)S(1)}, f32[2,128,512]{2,1,0:T(8,128)}) fusion(f32[2,128,256]{2,1,0:T(8,128)S(1)} %convert_add_fusion, f32[2,128,256]{2,1,0:T(8,128)S(1)} %collective-permute-done.11, pred[]{:T(512)S(6)} %eq.81), kind=kLoop, calls=%fused_computation.130 | loop fusion | flops 524288 | bytes 1572865 | tf_op jit(solution)/shard_map/mul | solution.py:117
  59.9 0.6 pad_maximum_fusion.3
  60.5 1.3 %collective-permute-start.12 = (f32[2,512]{1,0:T(2,128)}, f32[2,512]{1,0:T(2,128)}, u32[]{:S(2)}, u32[]{:S(2)}) collective-permute-start(f32[2,512]{1,0:T(2,128)} %pad_maximum_fusion.3), channel_id=1, source_target_pairs={{0,2},{2,0},{4,6},{6,4},{8,10},{10,8},{12,14},{14,12},{16,18},{18,... | collective-permute-start | bytes 12296 | tf_op jit(solution)/shard_map/ppermute | solution.py:120
  61.8 0.7 fusion.56
  62.5 2.0 %copy.24 = bf16[512,512]{1,0:T(8,128)(2,1)} copy(bf16[512,512]{0,1:T(8,128)(2,1)} %add_convert_fusion) | data formatting | bytes 1048576
  64.5 2.3 %collective-permute-start.3 = (bf16[64,512]{1,0:T(8,128)(2,1)}, bf16[64,512]{1,0:T(8,128)(2,1)S(1)}, u32[]{:S(2)}, u32[]{:S(2)}) collective-permute-start(bf16[64,512]{1,0:T(8,128)(2,1)} %get-tuple-element.16), channel_id=1, source_target_pairs={{30,0},{4,2},{2,4},{8,6},{6,8},{12,10},{10,12},{16,14},{14,16},{20... | collective-permute-start | bytes 196616 | tf_op jit(solution)/shard_map/ppermute | solution.py:195
  67.1 0.7 fusion.53
  67.7 0.7 collective-permute-start.13
  68.4 1.3 %fusion.6 = f32[128,512]{1,0:T(8,128)S(1)} fusion(f32[128,512]{1,0:T(8,128)S(1)} %fusion.26, f32[512,1536]{1,0:T(8,128)S(1)} %fusion.59, f32[320,512]{1,0:T(8,128)} %get-tuple-element.33, bf16[128,512]{1,0:T(8,128)(2,1)S(1)} %copy-done.8, s32[512]{0:T(512)S(1)} %copy-done.13), kind=kOutput, calls=%fused_computation.20 | convolution fusion | flops 68485120 | bytes 1968128 | tf_op jit(solution)/shard_map/dot_general | solution.py:48
  69.7 2.0 %collective-permute-done.13 = f32[2,512]{1,0:T(2,128)S(1)} collective-permute-done((f32[2,512]{1,0:T(2,128)S(1)}, f32[2,512]{1,0:T(2,128)S(1)}, u32[]{:S(2)}, u32[]{:S(2)}) %collective-permute-start.13) | collective-permute-done | bytes 4128 | tf_op jit(solution)/shard_map/ppermute | solution.py:120
  71.7 0.7 fusion.70
  72.4 0.8 collective-permute-start.14
  73.2 1.6 %fusion.8 = bf16[128,512]{1,0:T(8,128)(2,1)} fusion(f32[128,512]{1,0:T(8,128)S(1)} %fusion.6, bf16[1,64,512]{2,1,0:T(8,128)(2,1)S(1)} %bitcast.109, bf16[1,64,512]{2,1,0:T(8,128)(2,1)S(1)} %bitcast.108, bf16[1,64,512]{2,1,0:T(8,128)(2,1)S(1)} %bitcast.107, s32[3,64]{1,0:T(4,128)} %copy-done.14), kind=kOutput, calls=%fused_computation.23 | convolution fusion | flops 25518080 | bytes 590592 | tf_op jit(solution)/shard_map/khn,khd->nd/dot_general | solution.py:200
  74.9 1.2 %collective-permute-done.14 = f32[2,512]{1,0:T(2,128)S(1)} collective-permute-done((f32[2,512]{1,0:T(2,128)S(1)}, f32[2,512]{1,0:T(2,128)S(1)}, u32[]{:S(2)}, u32[]{:S(2)}) %collective-permute-start.14) | collective-permute-done | bytes 4128 | tf_op jit(solution)/shard_map/ppermute | solution.py:120
  76.0 1.3 %sqrt_reduce_fusion.1 = f32[]{:T(128)} fusion(f32[512]{0:T(512)S(1)} %bitcast.106, f32[512]{0:T(512)} %multiply_reduce_fusion), kind=kLoop, calls=%fused_computation.114 | loop fusion | flops 1535 | bytes 4100 | tf_op jit(solution)/shard_map/reduce_sum | solution.py:37
  78.0 0.7 multiply_divide_fusion.1
  78.6 0.6 sqrt_reduce_fusion
  79.9 1.6 %fusion.28 = f32[96,512]{1,0:T(8,128)} fusion(f32[2,128,512]{2,1,0:T(8,128)} %get-tuple-element.15, s32[]{:T(128)S(6)} %select_n.152, f32[512]{0:T(512)S(1)} %bitcast.102), kind=kLoop, calls=%fused_computation.70 | loop fusion | flops 49152 | bytes 395268 | tf_op jit(solution)/shard_map/mul | solution.py:41
  81.6 1.5 %fusion.41 = f32[32,512]{1,0:T(8,128)} fusion(f32[2,128,512]{2,1,0:T(8,128)} %get-tuple-element.15, s32[]{:T(128)S(6)} %select_n.152, s32[]{:T(128)S(6)} %add.250, f32[512]{0:T(512)S(1)} %bitcast.101), kind=kLoop, calls=%fused_computation.86 | loop fusion | flops 16384 | bytes 133128 | tf_op jit(solution)/shard_map/mul | solution.py:41
  (77 shorter events, 4.0 us)
Async XLA Ops:
  0.6 13.4 %copy-start.9 = (bf16[128,512]{1,0:T(8,128)(2,1)S(1)}, bf16[128,512]{1,0:T(8,128)(2,1)}, u32[]{:S(2)}) copy-start(bf16[128,512]{1,0:T(8,128)(2,1)} %param.11) | copy-start | bytes 393220
  0.6 12.4 %copy-start.15 = (bf16[512]{0:T(512)(128)(2,1)S(1)}, bf16[512]{0:T(512)(128)(2,1)}, u32[]{:S(2)}) copy-start(bf16[512]{0:T(512)(128)(2,1)} %param.15) | copy-start | bytes 3076
  0.7 12.5 %copy-start.16 = (bf16[512]{0:T(512)(128)(2,1)S(1)}, bf16[512]{0:T(512)(128)(2,1)}, u32[]{:S(2)}) copy-start(bf16[512]{0:T(512)(128)(2,1)} %param.17) | copy-start | bytes 3076
  0.7 12.5 %copy-start.17 = (bf16[512]{0:T(512)(128)(2,1)S(1)}, bf16[512]{0:T(512)(128)(2,1)}, u32[]{:S(2)}) copy-start(bf16[512]{0:T(512)(128)(2,1)} %param.18) | copy-start | bytes 3076
  1.5 8.2 %copy-start.14 = (s32[3,64]{1,0:T(4,128)}, s32[3,64]{1,0:T(4,128)S(1)}, u32[]{:S(2)}) copy-start(s32[3,64]{1,0:T(4,128)S(1)} %pad_add_fusion) | copy-start | bytes 2308
  2.7 12.0 %copy-start.2 = (bf16[1536,512]{1,0:T(8,128)(2,1)S(1)}, bf16[1536,512]{1,0:T(8,128)(2,1)}, u32[]{:S(2)}) copy-start(bf16[1536,512]{1,0:T(8,128)(2,1)} %param.14) | copy-start | bytes 4718596
  2.7 10.4 %collective-permute-start = (bf16[64,512]{1,0:T(8,128)(2,1)S(1)}, bf16[64,512]{1,0:T(8,128)(2,1)S(1)}, u32[]{:S(2)}, u32[]{:S(2)}) collective-permute-start(bf16[64,512]{1,0:T(8,128)(2,1)S(1)} %get-tuple-element.19), channel_id=1, source_target_pairs={{0,30},{2,4},{4,2},{6,8},{8,6},{10,12},{12,10},{14,16},{16,14},{18... | collective-permute-start | bytes 196616 | tf_op jit(solution)/shard_map/ppermute | solution.py:150
  9.8 4.3 %collective-permute-start.1 = (bf16[64,512]{1,0:T(8,128)(2,1)S(1)}, bf16[64,512]{1,0:T(8,128)(2,1)S(1)}, u32[]{:S(2)}, u32[]{:S(2)}) collective-permute-start(bf16[64,512]{1,0:T(8,128)(2,1)S(1)} %get-tuple-element.21), channel_id=1, source_target_pairs={{0,2},{2,0},{4,6},{6,4},{8,10},{10,8},{12,14},{14,12},{16,18},{18,... | collective-permute-start | bytes 196616 | tf_op jit(solution)/shard_map/ppermute | solution.py:150
  9.8 4.3 %collective-permute-start.2 = (bf16[64,512]{1,0:T(8,128)(2,1)S(1)}, bf16[64,512]{1,0:T(8,128)(2,1)S(1)}, u32[]{:S(2)}, u32[]{:S(2)}) collective-permute-start(bf16[64,512]{1,0:T(8,128)(2,1)S(1)} %get-tuple-element.20), channel_id=1, source_target_pairs={{0,1},{1,0},{2,3},{3,2},{4,5},{5,4},{6,7},{7,6},{8,9},{9,8},{10,11... | collective-permute-start | bytes 196616 | tf_op jit(solution)/shard_map/ppermute | solution.py:150
  13.1 2.6 %copy-start.11 = (bf16[512,512]{0,1:T(8,128)(2,1)}, bf16[512,512]{0,1:T(8,128)(2,1)S(1)}, u32[]{:S(2)}) copy-start(bf16[512,512]{0,1:T(8,128)(2,1)S(1)} %copy.18) | copy-start | bytes 1572868
  14.7 1.0 %copy-start.10 = (bf16[512,512]{1,0:T(8,128)(2,1)S(1)}, bf16[512,512]{1,0:T(8,128)(2,1)}, u32[]{:S(2)}) copy-start(bf16[512,512]{1,0:T(8,128)(2,1)} %param.16) | copy-start | bytes 1572868
  15.7 0.9 %copy-start.8 = (bf16[128,512]{1,0:T(8,128)(2,1)S(1)}, bf16[128,512]{1,0:T(8,128)(2,1)}, u32[]{:S(2)}) copy-start(bf16[128,512]{1,0:T(8,128)(2,1)} %param.13) | copy-start | bytes 393220
  15.7 0.9 %copy-start.13 = (s32[512]{0:T(512)S(1)}, s32[512]{0:T(512)}, u32[]{:S(2)}) copy-start(s32[512]{0:T(512)} %param.21) | copy-start | bytes 6148
  17.1 1.0 %copy-start.1 = (f32[512,512]{0,1:T(8,128)}, f32[512,512]{0,1:T(8,128)S(1)}, u32[]{:S(2)}) copy-start(f32[512,512]{0,1:T(8,128)S(1)} %get-tuple-element.31) | copy-start | bytes 3145732
  18.1 0.8 copy-start.6
  18.1 1.2 %copy-start.12 = (bf16[512,512]{0,1:T(8,128)(2,1)S(1)}, bf16[512,512]{0,1:T(8,128)(2,1)}, u32[]{:S(2)}) copy-start(bf16[512,512]{0,1:T(8,128)(2,1)} %copy-done.11) | copy-start | bytes 1572868
  20.3 1.6 %copy-start = (f32[1536,512]{1,0:T(8,128)}, f32[1536,512]{1,0:T(8,128)S(1)}, u32[]{:S(2)}) copy-start(f32[1536,512]{1,0:T(8,128)S(1)} %fusion.14) | copy-start | bytes 9437188
  22.0 2.8 %collective-permute-start.6 = (bf16[16,128,256]{2,1,0:T(8,128)(2,1)S(1)}, bf16[16,128,256]{2,1,0:T(8,128)(2,1)}, u32[]{:S(2)}, u32[]{:S(2)}) collective-permute-start(bf16[16,128,256]{2,1,0:T(8,128)(2,1)S(1)} %fusion.1), channel_id=1, source_target_pairs={{0,1},{1,0},{2,3},{3,2},{4,5},{5,4},{6,7},{7,6},{8,9},{9,8},{10,11... | collective-permute-start | bytes 3145736 | tf_op jit(solution)/shard_map/ppermute | solution.py:80
  26.9 9.2 %collective-permute-start.7 = (bf16[4,2,128,256]{3,2,0,1:T(8,128)(2,1)S(1)}, bf16[4,2,128,256]{3,2,0,1:T(8,128)(2,1)S(1)}, u32[]{:S(2)}, u32[]{:S(2)}) collective-permute-start(bf16[4,2,128,256]{3,2,0,1:T(8,128)(2,1)S(1)} %fusion.10), channel_id=1, source_target_pairs={{0,2},{1,5},{2,0},{3,7},{4,6},{5,1},{6,4},{7,3},{8,10},{9,13},{10,... | collective-permute-start | bytes 1572872 | tf_op jit(solution)/shard_map/ppermute | solution.py:93
  31.8 4.6 %copy-start.3 = (bf16[1536,512]{1,0:T(8,128)(2,1)S(1)}, bf16[1536,512]{1,0:T(8,128)(2,1)}, u32[]{:S(2)}) copy-start(bf16[1536,512]{1,0:T(8,128)(2,1)} %param.14) | copy-start | bytes 4718596
  31.8 4.6 %copy-start.7 = (bf16[512,512]{1,0:T(8,128)(2,1)S(1)}, bf16[512,512]{1,0:T(8,128)(2,1)}, u32[]{:S(2)}) copy-start(bf16[512,512]{1,0:T(8,128)(2,1)} %copy-done.6) | copy-start | bytes 1572868
  36.4 6.4 %collective-permute-start.8 = (bf16[4,128,256]{2,1,0:T(8,128)(2,1)S(1)}, bf16[4,128,256]{2,1,0:T(8,128)(2,1)S(1)}, u32[]{:S(2)}, u32[]{:S(2)}) collective-permute-start(bf16[4,128,256]{2,1,0:T(8,128)(2,1)S(1)} %fusion.25), channel_id=1, source_target_pairs={{0,4},{1,3},{2,6},{3,1},{4,0},{5,7},{6,2},{7,5},{8,12},{9,11},{10,... | collective-permute-start | bytes 786440 | tf_op jit(solution)/shard_map/ppermute | solution.py:93
  42.9 6.7 %copy-start.4 = (f32[4,128,256]{2,1,0:T(8,128)}, f32[4,128,256]{2,1,0:T(8,128)S(1)}, u32[]{:S(2)}) copy-start(f32[4,128,256]{2,1,0:T(8,128)S(1)} %bitcast_add_fusion) | copy-start | bytes 1572868
  42.9 5.0 %collective-permute-start.9 = (bf16[2,128,256]{2,1,0:T(8,128)(2,1)S(1)}, bf16[2,128,256]{2,1,0:T(8,128)(2,1)S(1)}, u32[]{:S(2)}, u32[]{:S(2)}) collective-permute-start(bf16[2,128,256]{2,1,0:T(8,128)(2,1)S(1)} %fusion.35), channel_id=1, source_target_pairs={{0,8},{1,9},{2,10},{3,11},{4,12},{5,13},{6,14},{7,15},{8,0},{9,1},... | collective-permute-start | bytes 393224 | tf_op jit(solution)/shard_map/ppermute | solution.py:93
  48.0 6.9 %collective-permute-start.10 = (bf16[2,128,256]{2,1,0:T(8,128)(2,1)S(1)}, bf16[2,128,256]{2,1,0:T(8,128)(2,1)}, u32[]{:S(2)}, u32[]{:S(2)}) collective-permute-start(bf16[2,128,256]{2,1,0:T(8,128)(2,1)S(1)} %fusion.34), channel_id=1, source_target_pairs={{0,16},{1,17},{2,18},{3,19},{4,20},{5,21},{6,22},{7,23},{8,24},{9,... | collective-permute-start | bytes 393224 | tf_op jit(solution)/shard_map/ppermute | solution.py:93
  55.9 3.0 %collective-permute-start.11 = (f32[2,128,256]{2,1,0:T(8,128)S(1)}, f32[2,128,256]{2,1,0:T(8,128)S(1)}, u32[]{:S(2)}, u32[]{:S(2)}) collective-permute-start(f32[2,128,256]{2,1,0:T(8,128)S(1)} %convert_add_fusion), channel_id=1, source_target_pairs={{0,1},{1,0},{2,3},{3,2},{4,5},{5,4},{6,7},{7,6},{8,9},{9,8},{10,11... | collective-permute-start | bytes 786440 | tf_op jit(solution)/shard_map/ppermute | solution.py:109
  58.5 3.3 %copy-start.5 = (bf16[320,512]{1,0:T(8,128)(2,1)S(1)}, bf16[320,512]{1,0:T(8,128)(2,1)}, u32[]{:S(2)}) copy-start(bf16[320,512]{1,0:T(8,128)(2,1)} %get-tuple-element.32) | copy-start | bytes 983044
  60.5 6.6 %collective-permute-start.12 = (f32[2,512]{1,0:T(2,128)}, f32[2,512]{1,0:T(2,128)}, u32[]{:S(2)}, u32[]{:S(2)}) collective-permute-start(f32[2,512]{1,0:T(2,128)} %pad_maximum_fusion.3), channel_id=1, source_target_pairs={{0,2},{2,0},{4,6},{6,4},{8,10},{10,8},{12,14},{14,12},{16,18},{18,... | collective-permute-start | bytes 12296 | tf_op jit(solution)/shard_map/ppermute | solution.py:120
  64.5 8.7 %collective-permute-start.3 = (bf16[64,512]{1,0:T(8,128)(2,1)}, bf16[64,512]{1,0:T(8,128)(2,1)S(1)}, u32[]{:S(2)}, u32[]{:S(2)}) collective-permute-start(bf16[64,512]{1,0:T(8,128)(2,1)} %get-tuple-element.16), channel_id=1, source_target_pairs={{30,0},{4,2},{2,4},{8,6},{6,8},{12,10},{10,12},{16,14},{14,16},{20... | collective-permute-start | bytes 196616 | tf_op jit(solution)/shard_map/ppermute | solution.py:195
  66.8 6.4 %collective-permute-start.4 = (bf16[64,512]{1,0:T(8,128)(2,1)}, bf16[64,512]{1,0:T(8,128)(2,1)S(1)}, u32[]{:S(2)}, u32[]{:S(2)}) collective-permute-start(bf16[64,512]{1,0:T(8,128)(2,1)} %get-tuple-element.18), channel_id=1, source_target_pairs={{2,0},{0,2},{6,4},{4,6},{10,8},{8,10},{14,12},{12,14},{18,16},{16,... | collective-permute-start | bytes 196616 | tf_op jit(solution)/shard_map/ppermute | solution.py:195
  66.8 6.4 %collective-permute-start.5 = (bf16[64,512]{1,0:T(8,128)(2,1)}, bf16[64,512]{1,0:T(8,128)(2,1)S(1)}, u32[]{:S(2)}, u32[]{:S(2)}) collective-permute-start(bf16[64,512]{1,0:T(8,128)(2,1)} %get-tuple-element.17), channel_id=1, source_target_pairs={{1,0},{0,1},{3,2},{2,3},{5,4},{4,5},{7,6},{6,7},{9,8},{8,9},{11,10... | collective-permute-start | bytes 196616 | tf_op jit(solution)/shard_map/ppermute | solution.py:195
  67.7 4.0 %collective-permute-start.13 = (f32[2,512]{1,0:T(2,128)S(1)}, f32[2,512]{1,0:T(2,128)S(1)}, u32[]{:S(2)}, u32[]{:S(2)}) collective-permute-start(f32[2,512]{1,0:T(2,128)S(1)} %fusion.53), channel_id=1, source_target_pairs={{0,4},{2,6},{4,0},{6,2},{8,12},{10,14},{12,8},{14,10},{16,20},{18,... | collective-permute-start | bytes 12296 | tf_op jit(solution)/shard_map/ppermute | solution.py:120
  72.4 3.6 %collective-permute-start.14 = (f32[2,512]{1,0:T(2,128)S(1)}, f32[2,512]{1,0:T(2,128)S(1)}, u32[]{:S(2)}, u32[]{:S(2)}) collective-permute-start(f32[2,512]{1,0:T(2,128)S(1)} %fusion.70), channel_id=1, source_target_pairs={{0,8},{2,10},{4,12},{6,14},{8,0},{10,2},{12,4},{14,6},{16,24},{18,... | collective-permute-start | bytes 12296 | tf_op jit(solution)/shard_map/ppermute | solution.py:120

commit v2 on v0

v2 whole, which is shorter than its diff:
```python
import functools
import math

import jax
import jax.numpy as jnp
from jax import lax
from jax.experimental import pallas as pl
from jax.experimental.pallas import tpu as pltpu
from jax.sharding import PartitionSpec as P

BF = jnp.bfloat16
F32 = jnp.float32


def halo_routes(axis, base, ring):
    count = lax.axis_size(axis)
    if count % 2:
        up = [(i, (i + 1) % count) for i in range(count) if ring or i + 1 < count]
        return [(up, base, base), ([(t, s) for s, t in up], base + 1, base + 1)]
    odd = lax.axis_index(axis) % 2
    near = [(i, i ^ 1) for i in range(count)]
    far = [(i, ((i + 1) ^ 1) - 1) for i in range(count)]
    far = [(s, t % count) for s, t in far if ring or 0 <= t < count]
    routes = [(near, base + odd, base + 1 - odd)]
    if far:
        routes.insert(0, (far, base + 1 - odd, base + odd))
    return routes


INNER = (((0,), (0,)), ((), ()))
OUTER = (((1,), (1,)), ((), ()))


def mm(left, right, dims=(((1,), (0,)), ((), ()))):
    return lax.dot_general(left, right, dims, preferred_element_type=F32)


def two_parts(values):
    high = values.astype(BF)
    return high, (values - high.astype(F32)).astype(BF)


def routes_of():
    routes = [("wide", r) for r in halo_routes("wide", 0, True)]
    return routes + [("narrow", r) for r in halo_routes("narrow", 2, False)]


def local_call(body, outs, args, gflops, far=0, scratch=()):
    vmem = pl.BlockSpec(memory_space=pltpu.VMEM)
    hbm = pl.BlockSpec(memory_space=pltpu.HBM)
    args = [
        pltpu.with_memory_space_constraint(value, pltpu.HBM) if i < far else value
        for i, value in enumerate(args)
    ]
    return pl.pallas_call(
        body,
        out_shape=outs,
        in_specs=[hbm] * far + [vmem] * (len(args) - far),
        out_specs=jax.tree.map(lambda _: vmem, outs),
        scratch_shapes=scratch,
        compiler_params=pltpu.CompilerParams(vmem_limit_bytes=VMEM_LIMIT),
        cost_estimate=pl.CostEstimate(
            flops=int(gflops * 1e9), bytes_accessed=1 << 20, transcendentals=0
        ),
    )(*args)


def fetch(sources, targets, sems):
    copies = [
        pltpu.make_async_copy(source, target, sems.at[i])
        for i, (source, target) in enumerate(zip(sources, targets))
    ]
    for copy in copies:
        copy.start()
    return copies


CHAINS = 2
VMEM_LIMIT = 24 * 1024 * 1024


def slot_hot(send_ref, block, node_count):
    slots = send_ref[0, pl.ds(block, 1), :]
    rows = lax.broadcasted_iota(jnp.int32, (node_count, slots.shape[1]), 0)
    return jnp.where(rows == slots, 1.0, 0.0).astype(BF)


def gather_body(send_hbm, node_hbm, send_ref, node_ref, *refs):
    *out_refs, sems = refs
    for copy in fetch((send_hbm, node_hbm), (send_ref, node_ref), sems):
        copy.wait()
    for (_, (_, sent, _)), out_ref in zip(routes_of(), out_refs):
        hot = slot_hot(send_ref, sent, node_ref.shape[0])
        out_ref[...] = mm(hot, node_ref[...], INNER).astype(BF)


def prepare_body(
    sender_hbm,
    receiver_hbm,
    cot_hbm,
    edge_hbm,
    w_first_hbm,
    w_second_hbm,
    node_ref,
    vectors_ref,
    start_ref,
    sender_hot_ref,
    receiver_hot_ref,
    edge_t_ref,
    up_ref,
    weight_sq_ref,
    cot_ref,
    w_first_ref,
    w_second_ref,
    sender_ref,
    receiver_ref,
    edge_ref,
    sems,
    *,
    slots,
):
    copies = fetch(
        (sender_hbm, receiver_hbm, cot_hbm, edge_hbm, w_first_hbm, w_second_hbm),
        (sender_ref, receiver_ref, cot_ref, edge_ref, w_first_ref, w_second_ref),
        sems,
    )
    nodes, width = node_ref.shape
    edges = edge_ref.shape[0]
    copies[0].wait()
    sender = sender_ref[...]
    row = sender
    for k, (_, (_, _, taken)) in enumerate(routes_of()):
        begin = nodes + taken * slots
        here = (sender >= begin) & (sender < begin + slots)
        row = jnp.where(here, sender - begin + (nodes + k * slots), row)
    table_rows = sender_hot_ref.shape[0]
    ids = lax.broadcasted_iota(jnp.int32, (table_rows, edges), 0)
    sender_hot_ref[...] = jnp.where(ids == row, 1.0, 0.0).astype(BF)
    copies[1].wait()
    ids = lax.broadcasted_iota(jnp.int32, (nodes, edges), 0)
    receiver_hot = jnp.where(ids == receiver_ref[...], 1.0, 0.0).astype(BF)
    receiver_hot_ref[...] = receiver_hot
    receiver_rows = mm(receiver_hot, node_ref[...], INNER).astype(BF)
    copies[2].wait()
    up_ref[...] = mm(receiver_hot, cot_ref[...], INNER).astype(BF)
    copies[3].wait()
    edge_t_ref[...] = edge_ref[...].T
    copies[4].wait()
    start_ref[...] = (
        mm(edge_ref[...], w_first_ref[:width])
        + mm(receiver_rows, w_first_ref[2 * width :])
        + vectors_ref[0:1]
    )
    first = w_first_ref[...].astype(F32)
    weight_sq_ref[0:1, :] = jnp.sum(first * first, 0, keepdims=True)
    copies[5].wait()
    second = w_second_ref[...].astype(F32)
    weight_sq_ref[1:2, :] = jnp.sum(second * second, 0, keepdims=True)


def middle_body(*refs, blocks, tile):
    (
        start_ref,
        sender_hot_ref,
        up_ref,
        node_ref,
        w_first_ref,
        w_second_ref,
        vectors_ref,
    ) = refs[:7]
    received = refs[7 : 7 + blocks]
    pre_back_ref, norm_back_ref, act_t_ref = refs[7 + blocks :]
    width = node_ref.shape[1]
    table = jnp.concatenate([node_ref[...]] + [r[...] for r in received], 0)
    bias, gain = vectors_ref[1:2], vectors_ref[2:3]
    for begin in range(0, start_ref.shape[0], tile):
        part = slice(begin, begin + tile)
        rows = mm(sender_hot_ref[:, part], table, INNER).astype(BF)
        preact = start_ref[part] + mm(rows, w_first_ref[width : 2 * width])
        sigma = 1.0 / (1.0 + jnp.exp(-preact))
        activation = (preact * sigma).astype(BF)
        act_t_ref[:, part] = activation.T
        second_pre = mm(activation, w_second_ref[...]) + bias
        centered = second_pre - jnp.mean(second_pre, -1, keepdims=True)
        variance = jnp.mean(centered * centered, -1, keepdims=True)
        inv_std = lax.rsqrt(variance + 1e-05)
        normalized = centered * inv_std
        scaled = up_ref[part].astype(F32) * gain
        norm_back = (
            inv_std
            * (
                scaled
                - jnp.mean(scaled, -1, keepdims=True)
                - normalized * jnp.mean(scaled * normalized, -1, keepdims=True)
            )
        ).astype(BF)
        norm_back_ref[part] = norm_back
        back = mm(norm_back, w_second_ref[...], OUTER)
        pre_back_ref[part] = (back * (sigma * (1.0 + preact * (1.0 - sigma)))).astype(BF)


def half_bit():
    narrow = lax.axis_size("narrow")
    return (lax.axis_index("narrow") // (narrow // 2)) % 2


def outer_body(*refs, blocks, own, chain):
    (edge_t_ref, act_t_ref, sender_hot_ref, receiver_hot_ref, pre_back_ref, norm_back_ref) = refs[:6]
    node_ref = refs[6]
    received = refs[7 : 7 + blocks]
    out_ref = refs[7 + blocks]
    span = out_ref.shape[2]
    half = half_bit() if own else 1 - half_bit()
    begin = pl.multiple_of(half * (CHAINS * span) + chain * span, span)
    columns = pl.ds(begin, span)
    pre_back = pre_back_ref[:, columns]
    node = node_ref[...]
    table = jnp.concatenate([node] + [r[...] for r in received], 0)
    by_sender = mm(sender_hot_ref[...], pre_back)
    by_receiver = mm(receiver_hot_ref[...], pre_back)
    high, low = two_parts(by_sender)
    high_r, low_r = two_parts(by_receiver)
    first = jnp.concatenate(
        [
            mm(edge_t_ref[...], pre_back),
            mm(table, high, INNER) + mm(table, low, INNER),
            mm(node, high_r, INNER) + mm(node, low_r, INNER),
        ],
        0,
    )
    second = mm(act_t_ref[...], norm_back_ref[:, columns])
    wide = out_ref.shape[0]
    first_rows = first.shape[0] // wide
    second_rows = second.shape[0] // wide
    for w in range(wide):
        out_ref[w, :first_rows] = first[w * first_rows : (w + 1) * first_rows].astype(out_ref.dtype)
        out_ref[w, first_rows:] = second[w * second_rows : (w + 1) * second_rows].astype(
            out_ref.dtype
        )


def back_body(*refs, blocks, slots):
    (pre_back_ref, w_first_ref, up_ref, cot_ref, sender_hot_ref, receiver_hot_ref) = refs[:6]
    edge_grad_ref, own_ref = refs[6:8]
    halo_refs = refs[8:]
    nodes, width = cot_ref.shape
    pre_back = pre_back_ref[...]
    high, low = two_parts(mm(sender_hot_ref[...], pre_back))
    weights = w_first_ref[width : 2 * width]
    table_grad = mm(high, weights, OUTER) + mm(low, weights, OUTER)
    for k, halo_ref in enumerate(halo_refs):
        begin = nodes + k * slots
        halo_ref[...] = table_grad[begin : begin + slots].astype(BF)
    high, low = two_parts(mm(receiver_hot_ref[...], pre_back))
    weights = w_first_ref[2 * width :]
    receiver_grad = mm(high, weights, OUTER) + mm(low, weights, OUTER)
    own_ref[...] = cot_ref[...].astype(F32) + table_grad[:nodes] + receiver_grad
    edge_grad_ref[...] = (
        up_ref[...].astype(F32) + mm(pre_back, w_first_ref[:width], OUTER)
    ).astype(BF)


def return_body(send_ref, own_ref, *refs):
    total = own_ref[...]
    for (_, (_, sent, _)), returned in zip(routes_of(), refs[:-1]):
        total += mm(slot_hot(send_ref, sent, total.shape[0]), returned[...])
    refs[-1][...] = total.astype(BF)


def combine_body(kept_ref, got_ref, next_ref, sent_ref, *, step):
    a = lax.axis_index("wide")
    odd = lax.axis_index("narrow") % 2
    low, high = a % 2, (a // 2) % 2
    for slot in range(next_ref.shape[0]):
        if step == 0:
            h, j = slot // 2, slot % 2
            kept = 4 * h + (1 - odd) * (2 * j + low) + odd * (2 * high + j)
            sent = 4 * h + (1 - odd) * (2 * j + 1 - low) + odd * (2 - 2 * high + j)
        elif step == 1:
            left = (1 - odd) * high + odd * low
            kept, sent = 2 * slot + left, 2 * slot + 1 - left
        else:
            bit = (a // (1 << step)) % 2
            kept, sent = 2 * slot + bit, 2 * slot + 1 - bit
        next_ref[slot] = kept_ref[kept] + got_ref[kept].astype(F32)
        sent_ref[slot] = (kept_ref[sent] + got_ref[sent].astype(F32)).astype(BF)


def whole_body(kept_ref, got_ref, next_ref, sent_ref):
    total = kept_ref[...] + got_ref[...].astype(F32)
    next_ref[...] = total
    sent_ref[...] = total.astype(BF)


def finish_body(kept_ref, got_ref, value_ref):
    value_ref[...] = kept_ref[...] + got_ref[...].astype(F32)


def sums_body(*refs, first_rows):
    value_ref, sums_ref = refs[2 * CHAINS :]
    for c in range(CHAINS):
        value = refs[c][...] + refs[CHAINS + c][...].astype(F32)
        columns = slice(c * value.shape[2], (c + 1) * value.shape[2])
        value_ref[:, :, columns] = value
        value = value * value
        sums_ref[0:1, columns] = jnp.sum(jnp.sum(value[:, :first_rows], 0), 0, keepdims=True)
        sums_ref[1:2, columns] = jnp.sum(jnp.sum(value[:, first_rows:], 0), 0, keepdims=True)


def clip_body(own_ref, other_ref, sums_ref, other_sums_ref, weight_sq_ref, first_ref, second_ref, *, top):
    half = half_bit()
    span = own_ref.shape[2]
    first_rows = first_ref.shape[0]
    share = lax.axis_index("wide") // top
    width = 2 * span
    wide = lax.axis_size("wide")
    columns = (
        pl.ds(pl.multiple_of(half * span, span), span),
        pl.ds(pl.multiple_of((1 - half) * span, span), span),
    )
    sums = (sums_ref[...] + 1e-06, other_sums_ref[...] + 1e-06)
    weight = [weight_sq_ref[:, c] + 1e-06 for c in columns]
    total = sum(jnp.sum(jnp.sqrt(s / w), 1, keepdims=True) for s, w in zip(sums, weight))
    mean_ratio = total / width
    fans = (first_ref.shape[0] * wide, second_ref.shape[0] * wide)
    for c, s, w, value_ref in zip(columns, sums, weight, (own_ref, other_ref)):
        factor = jnp.minimum(1.0 / (mean_ratio * jnp.sqrt(w)), 1.0 / jnp.sqrt(s))
        value = value_ref[share]
        first_ref[:, c] = value[:first_rows] * (factor[0:1] * math.sqrt(fans[0]))
        second_ref[:, c] = value[first_rows:] * (factor[1:2] * math.sqrt(fans[1]))


def swap_pairs(size, mask):
    return [(i, i ^ mask) for i in range(size)]


def crossed(value, even_mask, odd_mask):
    wide, narrow = lax.axis_size("wide"), lax.axis_size("narrow")
    pairs = []
    for i in range(wide):
        for j in range(narrow):
            pairs.append((i * narrow + j, (i ^ (odd_mask if j % 2 else even_mask)) * narrow + j))
    return lax.ppermute(value, ("wide", "narrow"), pairs)


def per_device(
    node_latent,
    edge_latent,
    node_cotangent,
    w_first,
    bias_first,
    w_second,
    bias_second,
    norm_gain,
    send_map,
    edge_sender,
    edge_receiver,
):
    nodes, width = node_latent.shape
    edges = edge_latent.shape[0]
    slots = send_map.shape[2]
    wide, narrow = lax.axis_size("wide"), lax.axis_size("narrow")
    if wide < 4 or wide & (wide - 1) or narrow < 2 or narrow & (narrow - 1):
        raise ValueError("axis sizes")
    routes = routes_of()
    blocks = len(routes)
    table_rows = nodes + blocks * slots

    def like(shape, kind):
        return jax.ShapeDtypeStruct(shape, kind)

    halo = [like((slots, width), BF)] * blocks
    send_slots, node, *outgoing = local_call(
        gather_body,
        [like(send_map.shape, jnp.int32), like((nodes, width), BF), *halo],
        (send_map, node_latent),
        0.1,
        far=2,
        scratch=[pltpu.SemaphoreType.DMA((2,))],
    )
    received = [
        lax.ppermute(block, axis, pairs) for block, (axis, (pairs, _, _)) in zip(outgoing, routes)
    ]
    vectors = jnp.stack([v.astype(F32) for v in (bias_first, bias_second, norm_gain)], 0)
    start, sender_hot, receiver_hot, edge_t, up, weight_sq, cot, weights, weights_2 = local_call(
        functools.partial(prepare_body, slots=slots),
        [
            like((edges, width), F32),
            like((table_rows, edges), BF),
            like((nodes, edges), BF),
            like((width, edges), BF),
            like((edges, width), BF),
            like((2, width), F32),
            like((nodes, width), BF),
            like(w_first.shape, BF),
            like(w_second.shape, BF),
        ],
        (
            edge_sender.reshape(1, edges),
            edge_receiver.reshape(1, edges),
            node_cotangent,
            edge_latent,
            w_first,
            w_second,
            node,
            vectors,
        ),
        1.0,
        far=6,
        scratch=[
            pltpu.VMEM((1, edges), jnp.int32),
            pltpu.VMEM((1, edges), jnp.int32),
            pltpu.VMEM((edges, width), BF),
            pltpu.SemaphoreType.DMA((6,)),
        ],
    )
    pre_back, norm_back, act_t = local_call(
        functools.partial(middle_body, blocks=blocks, tile=edges // 2),
        [like((edges, width), BF), like((edges, width), BF), like((width, edges), BF)],
        (start, sender_hot, up, node, weights, weights_2, vectors, *received),
        1.0,
    )
    first_rows, second_rows = w_first.shape[0] // wide, w_second.shape[0] // wide
    rows = first_rows + second_rows
    span = width // 2 // CHAINS
    operands = (edge_t, act_t, sender_hot, receiver_hot, pre_back, norm_back, node, *received)

    def outer(own, chain, kind):
        (grad,) = local_call(
            functools.partial(outer_body, blocks=blocks, own=own, chain=chain),
            [like((wide, rows, span), kind)],
            operands,
            0.6 / CHAINS,
        )
        return grad

    half_swap = swap_pairs(narrow, narrow // 2)
    gots = [lax.ppermute(outer(False, c, BF), "narrow", half_swap) for c in range(CHAINS)]
    kepts = [outer(True, c, F32) for c in range(CHAINS)]
    edge_grad, own_grad, *halo_grad = local_call(
        functools.partial(back_body, blocks=blocks, slots=slots),
        [like((edges, width), BF), like((nodes, width), F32), *halo],
        (pre_back, weights, up, cot, sender_hot, receiver_hot),
        1.0,
    )
    mask = narrow // 4
    while mask:
        span //= 2
        bit = (lax.axis_index("narrow") // mask) % 2
        for c in range(CHAINS):
            value = kepts[c] + gots[c].astype(F32)
            sent = lax.dynamic_slice_in_dim(value, (1 - bit) * span, span, 2).astype(BF)
            kepts[c] = lax.dynamic_slice_in_dim(value, bit * span, span, 2)
            gots[c] = lax.ppermute(sent, "narrow", swap_pairs(narrow, mask))
        mask //= 2
    bits = wide.bit_length() - 1
    for step in range(bits - 1):
        shape = (wide >> (step + 1), rows, span)
        masks = [(1, 2), (2, 1)][step] if step < 2 else (1 << step, 1 << step)
        for c in range(CHAINS):
            kepts[c], sent = local_call(
                functools.partial(combine_body, step=step),
                [like(shape, F32), like(shape, BF)],
                (kepts[c], gots[c]),
                0.01,
            )
            gots[c] = crossed(sent, *masks)
        if step == 0:
            gots[-1], halo_grad = lax.optimization_barrier((gots[-1], halo_grad))
            returned = [
                lax.ppermute(block, axis, [(t, s) for s, t in pairs])
                for block, (axis, (pairs, _, _)) in zip(halo_grad, routes)
            ]
        if step == bits - 2:
            gots[-1], returned = lax.optimization_barrier((gots[-1], returned))
    (node_grad,) = local_call(
        return_body, [like((nodes, width), BF)], (send_slots, own_grad, *returned), 0.1
    )
    top = wide // 2
    shape = (2, rows, span)
    for c in range(CHAINS):
        kepts[c], sent = local_call(
            whole_body, [like(shape, F32), like(shape, BF)], (kepts[c], gots[c]), 0.01
        )
        gots[c] = crossed(sent, top, top)
        if narrow > 2:
            (value,) = local_call(finish_body, [like(shape, F32)], (kepts[c], gots[c]), 0.01)
            mask = 1
            while mask < narrow // 2:
                other = lax.ppermute(value, "narrow", swap_pairs(narrow, mask))
                value = jnp.where(
                    (lax.axis_index("narrow") // mask) % 2 == 0,
                    jnp.concatenate([value, other], 2),
                    jnp.concatenate([other, value], 2),
                )
                mask *= 2
            kepts[c], gots[c] = value, jnp.zeros(value.shape, BF)
    value, sums = local_call(
        functools.partial(sums_body, first_rows=first_rows),
        [like((2, rows, width // 2), F32), like((2, width // 2), F32)],
        (*kepts, *gots),
        0.001,
    )
    other = lax.ppermute(value, "narrow", half_swap)
    for position in range(bits - 1):
        sums = sums + lax.ppermute(sums, "wide", swap_pairs(wide, 1 << position))
    other_sums = lax.ppermute(sums, "narrow", half_swap)
    first_update, second_update = local_call(
        functools.partial(clip_body, top=top),
        [like((first_rows, width), F32), like((second_rows, width), F32)],
        (value, other, sums, other_sums, weight_sq),
        0.001,
    )
    return (node_grad, edge_grad, first_update, second_update)


def solution(mesh):
    return jax.shard_map(
        per_device,
        mesh=mesh,
        in_specs=(
            P(("wide", "narrow"), None),
            P(("wide", "narrow"), None),
            P(("wide", "narrow"), None),
            P(),
            P(),
            P(),
            P(),
            P(),
            P(("wide", "narrow"), None, None),
            P(("wide", "narrow")),
            P(("wide", "narrow")),
        ),
        out_specs=(
            P(("wide", "narrow"), None),
            P(("wide", "narrow"), None),
            P("wide", None),
            P("wide", None),
        ),
        check_vma=False,
    )
```

time: 193 us -> 61.5 us (0.32)
  waiting for transfers between devices: 119 us -> 24.2 us
  matrix products: 18.9 us -> 0 us
  between operations: 15.6 us -> 0.81 us
  Pallas kernels: 0 us -> 14.3 us
  other arithmetic: 11.6 us -> 0.03 us
  local copies, waits for them, and re-layouts: 7.15 us -> 2.05 us
    psum x1 -> x0, waiting for transfers between devices: 116 us -> none  [per_device(): lax.psum((first_grad, second_grad), ('wide', 'narrow'))]
    ppermute x8 -> x21, waiting for transfers between devices: 3.22 us -> 24.2 us  [the longest x8 11.7 us: crossed(): return lax.ppermute(value, ('wide', 'narrow'), pairs)]
    dot_general x13 -> x0, matrix products: 18.9 us -> none  [the longest x2 4.11 us: edge_contract(): lax.dot_general(hot_table, values, (((0,), (0,)), ((), ())), precision=la...]
    pallas_call x0 -> x19, Pallas kernels: none -> 14.3 us  [local_call(): pl.pallas_call(body, out_shape=outs, in_specs=[hbm] * far + [vmem] * (len...]
    unnamed x23 -> x0, local copies, waits for them, and re-layouts: 6.07 us -> none
    convert_element_type x5 -> x0, other arithmetic: 4.89 us -> none  [the longest x1 2.55 us: per_device(): edge_grad = (upstream + input_back[:, :feature_width]).astype(jnp.bfloat16)]
    reduce_sum x7 -> x0, other arithmetic: 4.34 us -> none  [the longest x1 2.26 us: per_device(): first_grad_sq = jnp.sum(first_total * first_total, 0)]
    mul x2 -> x0, other arithmetic: 2.27 us -> none  [clip_share(): return grad_share * factor * math.sqrt(fan_rows)]
  transfers between devices with their start and end apart: 9 -> 21, of which waited for: 2 -> 12; matrix products, arithmetic and copies ran while one was open for 12% -> 3% of each run, Pallas kernels for 0% -> 14%
where the time goes in v2:
time: 61.5 us; the launch traced here: 61.3 us
  waiting for transfers between devices  24.2 us (39%)
  starting transfers between devices  19.9 us (32%)
  Pallas kernels  14.3 us (23%)
  local copies, waits for them, and re-layouts  2.05 us (3%)
  between operations  0.81 us (1%)
    pallas_call x19, Pallas kernels, local_call(): pl.pallas_call(body, out_shape=outs, in_specs=[hbm] * far + [vmem] * (len...  14.3 us
    ppermute x8, waiting for transfers between devices, crossed(): return lax.ppermute(value, ('wide', 'narrow'), pairs)  11.7 us
    ppermute x3, waiting for transfers between devices, per_device(): sums = sums + lax.ppermute(sums, 'wide', swap_pairs(wide, 1 << position))  9.58 us
    ppermute x8, starting transfers between devices, crossed(): return lax.ppermute(value, ('wide', 'narrow'), pairs)  7.39 us
    ppermute x3, starting transfers between devices, per_device(): lax.ppermute(block, axis, pairs)  7.03 us
    ppermute x3, starting transfers between devices, per_device(): lax.ppermute(block, axis, [(t, s) for s, t in pairs])  3.51 us
    ppermute x3, waiting for transfers between devices, per_device(): lax.ppermute(block, axis, [(t, s) for s, t in pairs])  2.6 us
    another operation x3, local copies, waits for them, and re-layouts, per_device(): jnp.stack([v.astype(F32) for v in (bias_first, bias_second, norm_gain)], 0)  2.05 us
  transfers between devices with their start and end apart: 21, of which 12 were waited for; matrix products, arithmetic and copies ran while one was open for 3% of the time, Pallas kernels for 14%

profile of v2, /device:TPU:0, one launch (start us, length us, event | category | flops | bytes accessed | tf_op | source)
XLA Modules:
  0.0 61.3 jit_solution(1170547495383347269)
XLA Ops:
  0.6 1.2 %shard_map.138 = (s32[1,4,64]{2,1,0:T(4,128)S(1)}, bf16[128,512]{1,0:T(8,128)(2,1)S(1)}, bf16[64,512]{1,0:T(8,128)(2,1)S(1)}, bf16[64,512]{1,0:T(8,128)(2,1)S(1)}, bf16[64,512]{1,0:T(8,128)(2,1)S(1)}) custom-call(s32[1,4,64]{2,1,0:T(4,128)} %send_hbm.1, bf16[128,512]{1,0:T(8,128)(2,1)} %node_hbm.1), custom_call_target="tpu_custom_call" | custom-call | flops 100000000 | bytes 1048576 | tf_op jit(solution)/shard_map/pallas_call | solution.py:55
  1.8 7.0 %collective-permute-start = (bf16[64,512]{1,0:T(8,128)(2,1)S(1)}, bf16[64,512]{1,0:T(8,128)(2,1)S(1)}, u32[]{:S(2)}, u32[]{:S(2)}) collective-permute-start(bf16[64,512]{1,0:T(8,128)(2,1)S(1)} %get-tuple-element.61), channel_id=1, source_target_pairs={{0,30},{2,4},{4,2},{6,8},{8,6},{10,12},{12,10},{14,16},{16,14},{18... | collective-permute-start | bytes 196616 | tf_op jit(solution)/shard_map/ppermute | solution.py:382
  8.9 0.0 collective-permute-start.1
  8.9 0.7 %stack.19 = bf16[1,512]{1,0:T(2,128)(2,1)S(1)} reshape(bf16[512]{0:T(512)(128)(2,1)} %param.18) | data formatting | bytes 2048 | tf_op jit(solution)/shard_map/stack | solution.py:384
  9.5 0.7 %stack.18 = bf16[1,512]{1,0:T(2,128)(2,1)S(1)} reshape(bf16[512]{0:T(512)(128)(2,1)} %param.17) | data formatting | bytes 2048 | tf_op jit(solution)/shard_map/stack | solution.py:384
  10.2 0.7 %stack.17 = bf16[1,512]{1,0:T(2,128)(2,1)S(1)} reshape(bf16[512]{0:T(512)(128)(2,1)} %param.15) | data formatting | bytes 2048 | tf_op jit(solution)/shard_map/stack | solution.py:384
  10.9 2.5 %shard_map.139 = (f32[512,512]{1,0:T(8,128)S(1)}, bf16[320,512]{1,0:T(8,128)(2,1)S(1)}, bf16[128,512]{1,0:T(8,128)(2,1)S(1)}, bf16[512,512]{1,0:T(8,128)(2,1)S(1...) custom-call(s32[1,512]{1,0:T(1,128)} %bitcast.2, ...), custom_call_target="tpu_custom_call" | custom-call | flops 1000000000 | bytes 1048576 | tf_op jit(solution)/shard_map/pallas_call | solution.py:55
  13.4 0.0 collective-permute-done.refs_7_
  13.4 0.0 collective-permute-done.1.refs_8_
  13.5 2.6 %shard_map.140 = (bf16[512,512]{1,0:T(8,128)(2,1)S(1)}, bf16[512,512]{1,0:T(8,128)(2,1)S(1)}, bf16[512,512]{1,0:T(8,128)(2,1)S(1)}) custom-call(f32[512,512]{1,0:T(8,128)S(1)} %get-tuple-element.56.refs_0_, bf16[320,512]{1,0:T(8,128)(2,1)S(1)} %get-tuple-element.57.refs_1_.refs_4_.refs_2_, bf16[512,512]{1,0:T(8,128)(2,1)S(1)} %get-tuple-element.58.refs_2_, ...), custom_call_target="tpu_custom_call" | custom-call | flops 1000000000 | bytes 1048576 | tf_op jit(solution)/shard_map/pallas_call | solution.py:55
  16.1 0.9 %shard_map.143 = bf16[16,128,128]{2,1,0:T(8,128)(2,1)S(1)} custom-call(bf16[512,512]{1,0:T(8,128)(2,1)S(1)} %get-tuple-element.68.refs_0_, bf16[512,512]{1,0:T(8,128)(2,1)S(1)} %get-tuple-element.69.refs_1_, bf16[320,512]{1,0:T(8,128)(2,1)S(1)} %get-tuple-element.57.refs_1_.refs_4_.refs_2_, bf16[128,512]{1,0:T(8,128)(2,1)S(1)} %get-tuple-element.66.refs_5_.refs_3_, ...), custom_call_target="tpu_custom_call" | custom-call | flops 300000000 | bytes 1048576 | tf_op jit(solution)/shard_map/pallas_call | solution.py:55
  16.9 0.6 collective-permute-start.3
  17.5 0.9 %shard_map.149 = bf16[16,128,128]{2,1,0:T(8,128)(2,1)S(1)} custom-call(bf16[512,512]{1,0:T(8,128)(2,1)S(1)} %get-tuple-element.68.refs_0_, bf16[512,512]{1,0:T(8,128)(2,1)S(1)} %get-tuple-element.69.refs_1_, bf16[320,512]{1,0:T(8,128)(2,1)S(1)} %get-tuple-element.57.refs_1_.refs_4_.refs_2_, bf16[128,512]{1,0:T(8,128)(2,1)S(1)} %get-tuple-element.66.refs_5_.refs_3_, ...), custom_call_target="tpu_custom_call" | custom-call | flops 300000000 | bytes 1048576 | tf_op jit(solution)/shard_map/pallas_call | solution.py:55
  18.4 0.1 collective-permute-start.10
  18.5 0.9 %shard_map.142.kept_ref = f32[16,128,128]{2,1,0:T(8,128)S(1)} custom-call(bf16[512,512]{1,0:T(8,128)(2,1)S(1)} %get-tuple-element.68.refs_0_, bf16[512,512]{1,0:T(8,128)(2,1)S(1)} %get-tuple-element.69.refs_1_, bf16[320,512]{1,0:T(8,128)(2,1)S(1)} %get-tuple-element.57.refs_1_.refs_4_.refs_2_, bf16[128,512]{1,0:T(8,128)(2,1)S(1)} %get-tuple-element.66.refs_5_.refs_3_, ...), custom_call_target="tpu_custom_call" | custom-call | flops 300000000 | bytes 1048576 | tf_op jit(solution)/shard_map/pallas_call | solution.py:55
  19.4 0.1 shard_map.144
  19.5 2.1 %collective-permute-start.4 = (bf16[8,128,128]{2,1,0:T(8,128)(2,1)S(1)}, bf16[8,128,128]{2,1,0:T(8,128)(2,1)S(1)}, u32[]{:S(2)}, u32[]{:S(2)}) collective-permute-start(bf16[8,128,128]{2,1,0:T(8,128)(2,1)S(1)} %get-tuple-element.72), channel_id=1, source_target_pairs={{0,2},{1,5},{2,0},{3,7},{4,6},{5,1},{6,4},{7,3},{8,10},{9,13},{10,... | collective-permute-start | bytes 786440 | tf_op jit(solution)/shard_map/ppermute | solution.py:343
  21.6 0.9 %shard_map.148.kept_ref = f32[16,128,128]{2,1,0:T(8,128)S(1)} custom-call(bf16[512,512]{1,0:T(8,128)(2,1)S(1)} %get-tuple-element.68.refs_0_, bf16[512,512]{1,0:T(8,128)(2,1)S(1)} %get-tuple-element.69.refs_1_, bf16[320,512]{1,0:T(8,128)(2,1)S(1)} %get-tuple-element.57.refs_1_.refs_4_.refs_2_, bf16[128,512]{1,0:T(8,128)(2,1)S(1)} %get-tuple-element.66.refs_5_.refs_3_, ...), custom_call_target="tpu_custom_call" | custom-call | flops 300000000 | bytes 1048576 | tf_op jit(solution)/shard_map/pallas_call | solution.py:55
  22.4 0.1 shard_map.150
  22.6 0.1 collective-permute-start.11
  22.7 2.3 %shard_map.141 = (bf16[512,512]{1,0:T(8,128)(2,1)}, f32[128,512]{1,0:T(8,128)S(1)}, bf16[64,512]{1,0:T(8,128)(2,1)S(1)}, bf16[64,512]{1,0:T(8,128)(2,1)S(1)}, bf16[64,512]{1,0:T(8,128)(2,1)S(1)}) custom-call(bf16[512,512]{1,0:T(8,128)(2,1)S(1)} %get-tuple-element.64.refs_0_.refs_4_, bf16[1536,512]{1,0:T(8,128)(2,1)S(1)} %get-tuple-element.59.refs_4_.refs_1_, ...), custom_call_target="tpu_custom_call" | custom-call | flops 1000000000 | bytes 1048576 | tf_op jit(solution)/shard_map/pallas_call | solution.py:55
  25.0 0.9 %collective-permute-done.4.got_ref = bf16[8,128,128]{2,1,0:T(8,128)(2,1)S(1)} collective-permute-done((bf16[8,128,128]{2,1,0:T(8,128)(2,1)S(1)}, bf16[8,128,128]{2,1,0:T(8,128)(2,1)S(1)}, u32[]{:S(2)}, u32[]{:S(2)}) %collective-permute-start.4) | collective-permute-done | bytes 262176 | tf_op jit(solution)/shard_map/ppermute | solution.py:343
  25.9 0.1 shard_map.145
  26.0 0.1 collective-permute-start.5
  26.1 3.4 %collective-permute-done.11.got_ref = bf16[8,128,128]{2,1,0:T(8,128)(2,1)S(1)} collective-permute-done((bf16[8,128,128]{2,1,0:T(8,128)(2,1)S(1)}, bf16[8,128,128]{2,1,0:T(8,128)(2,1)S(1)}, u32[]{:S(2)}, u32[]{:S(2)}) %collective-permute-start.11) | collective-permute-done | bytes 262176 | tf_op jit(solution)/shard_map/ppermute | solution.py:343
  29.4 0.1 shard_map.151
  29.5 0.1 collective-permute-start.12
  29.6 3.5 %collective-permute-start.7 = (bf16[64,512]{1,0:T(8,128)(2,1)S(1)}, bf16[64,512]{1,0:T(8,128)(2,1)S(1)}, u32[]{:S(2)}, u32[]{:S(2)}) collective-permute-start(bf16[64,512]{1,0:T(8,128)(2,1)S(1)} %get-tuple-element.80), channel_id=1, source_target_pairs={{30,0},{4,2},{2,4},{8,6},{6,8},{12,10},{10,12},{16,14},{14,16},{20... | collective-permute-start | bytes 196616 | tf_op jit(solution)/shard_map/ppermute | solution.py:471
  33.1 1.2 %collective-permute-start.6 = (bf16[2,128,128]{2,1,0:T(8,128)(2,1)S(1)}, bf16[2,128,128]{2,1,0:T(8,128)(2,1)S(1)}, u32[]{:S(2)}, u32[]{:S(2)}) collective-permute-start(bf16[2,128,128]{2,1,0:T(8,128)(2,1)S(1)} %get-tuple-element.79), channel_id=1, source_target_pairs={{0,8},{1,9},{2,10},{3,11},{4,12},{5,13},{6,14},{7,15},{8,0},{9,1},... | collective-permute-start | bytes 196616 | tf_op jit(solution)/shard_map/ppermute | solution.py:343
  34.4 0.1 collective-permute-done.12.got_ref
  34.6 0.8 %collective-permute-start.13 = (bf16[2,128,128]{2,1,0:T(8,128)(2,1)S(1)}, bf16[2,128,128]{2,1,0:T(8,128)(2,1)S(1)}, u32[]{:S(2)}, u32[]{:S(2)}) collective-permute-start(bf16[2,128,128]{2,1,0:T(8,128)(2,1)S(1)} %get-tuple-element.92), channel_id=1, source_target_pairs={{0,8},{1,9},{2,10},{3,11},{4,12},{5,13},{6,14},{7,15},{8,0},{9,1},... | collective-permute-start | bytes 196616 | tf_op jit(solution)/shard_map/ppermute | solution.py:343
  35.3 2.6 %collective-permute-done.7.refs_0_ = bf16[64,512]{1,0:T(8,128)(2,1)S(1)} collective-permute-done((bf16[64,512]{1,0:T(8,128)(2,1)S(1)}, bf16[64,512]{1,0:T(8,128)(2,1)S(1)}, u32[]{:S(2)}, u32[]{:S(2)}) %collective-permute-start.7) | collective-permute-done | bytes 65568 | tf_op jit(solution)/shard_map/ppermute | solution.py:471
  37.9 0.2 collective-permute-done.6.got_ref
  38.2 1.1 %collective-permute-done.13.got_ref = bf16[2,128,128]{2,1,0:T(8,128)(2,1)S(1)} collective-permute-done((bf16[2,128,128]{2,1,0:T(8,128)(2,1)S(1)}, bf16[2,128,128]{2,1,0:T(8,128)(2,1)S(1)}, u32[]{:S(2)}, u32[]{:S(2)}) %collective-permute-start.13) | collective-permute-done | bytes 65568 | tf_op jit(solution)/shard_map/ppermute | solution.py:343
  39.3 0.2 collective-permute-start.14
  39.5 2.9 %collective-permute-start.15 = (bf16[2,128,128]{2,1,0:T(8,128)(2,1)S(1)}, bf16[2,128,128]{2,1,0:T(8,128)(2,1)S(1)}, u32[]{:S(2)}, u32[]{:S(2)}) collective-permute-start(bf16[2,128,128]{2,1,0:T(8,128)(2,1)S(1)} %get-tuple-element.98), channel_id=1, source_target_pairs={{0,16},{1,17},{2,18},{3,19},{4,20},{5,21},{6,22},{7,23},{8,24},{9,... | collective-permute-start | bytes 196616 | tf_op jit(solution)/shard_map/ppermute | solution.py:343
  42.4 5.0 %collective-permute-done.14.refs_2_ = bf16[2,128,128]{2,1,0:T(8,128)(2,1)S(1)} collective-permute-done((bf16[2,128,128]{2,1,0:T(8,128)(2,1)S(1)}, bf16[2,128,128]{2,1,0:T(8,128)(2,1)S(1)}, u32[]{:S(2)}, u32[]{:S(2)}) %collective-permute-start.14) | collective-permute-done | bytes 65568 | tf_op jit(solution)/shard_map/ppermute | solution.py:343
  47.4 1.0 %collective-permute-done.15.refs_3_ = bf16[2,128,128]{2,1,0:T(8,128)(2,1)S(1)} collective-permute-done((bf16[2,128,128]{2,1,0:T(8,128)(2,1)S(1)}, bf16[2,128,128]{2,1,0:T(8,128)(2,1)S(1)}, u32[]{:S(2)}, u32[]{:S(2)}) %collective-permute-start.15) | collective-permute-done | bytes 65568 | tf_op jit(solution)/shard_map/ppermute | solution.py:343
  48.3 0.1 shard_map.155
  48.4 0.1 collective-permute-start.16
  48.5 1.2 %collective-permute-start.17 = (f32[2,256]{1,0:T(2,128)S(1)}, f32[2,256]{1,0:T(2,128)S(1)}, u32[]{:S(2)}, u32[]{:S(2)}) collective-permute-start(f32[2,256]{1,0:T(2,128)S(1)} %get-tuple-element.100), channel_id=1, source_target_pairs={{0,2},{2,0},{4,6},{6,4},{8,10},{10,8},{12,14},{14,12},{16,18},{18,... | collective-permute-start | bytes 6152 | tf_op jit(solution)/shard_map/ppermute | solution.py:506
  49.6 2.5 %collective-permute-done.17 = f32[2,256]{1,0:T(2,128)S(1)} collective-permute-done((f32[2,256]{1,0:T(2,128)S(1)}, f32[2,256]{1,0:T(2,128)S(1)}, u32[]{:S(2)}, u32[]{:S(2)}) %collective-permute-start.17) | collective-permute-done | bytes 2080 | tf_op jit(solution)/shard_map/ppermute | solution.py:506
  52.1 0.0 collective-permute-start.18
  52.2 3.5 %collective-permute-done.18 = f32[2,256]{1,0:T(2,128)S(1)} collective-permute-done((f32[2,256]{1,0:T(2,128)S(1)}, f32[2,256]{1,0:T(2,128)S(1)}, u32[]{:S(2)}, u32[]{:S(2)}) %collective-permute-start.18) | collective-permute-done | bytes 2080 | tf_op jit(solution)/shard_map/ppermute | solution.py:506
  55.7 3.6 %collective-permute-done.19 = f32[2,256]{1,0:T(2,128)S(1)} collective-permute-done((f32[2,256]{1,0:T(2,128)S(1)}, f32[2,256]{1,0:T(2,128)S(1)}, u32[]{:S(2)}, u32[]{:S(2)}) %collective-permute-start.19) | collective-permute-done | bytes 2080 | tf_op jit(solution)/shard_map/ppermute | solution.py:506
  59.3 0.9 %shard_map.147 = bf16[128,512]{1,0:T(8,128)(2,1)} custom-call(s32[1,4,64]{2,1,0:T(4,128)S(1)} %get-tuple-element.54.send_ref, f32[128,512]{1,0:T(8,128)S(1)} %get-tuple-element.67.own_ref, bf16[64,512]{1,0:T(8,128)(2,1)S(1)} %collective-permute-done.7.refs_0_, bf16[64,512]{1,0:T(8,128)(2,1)S(1)} %collective-permute-done.8.refs_1_, ...), custom_call_target="tpu_custom_call" | custom-call | flops 100000000 | bytes 1048576 | tf_op jit(solution)/shard_map/pallas_call | solution.py:55
  60.2 0.3 collective-permute-done.20.other_sums_ref
  60.5 0.8 %shard_map.156 = (f32[96,512]{1,0:T(8,128)}, f32[32,512]{1,0:T(8,128)}) custom-call(f32[2,128,256]{2,1,0:T(8,128)S(1)} %get-tuple-element.99.own_ref, f32[2,128,256]{2,1,0:T(8,128)S(1)} %collective-permute-done.16.other_ref, f32[2,256]{1,0:T(2,128)S(1)} %add.11.sums_ref, f32[2,256]{1,0:T(2,128)S(1)} %collective-permute-done.20.other_sums_ref, ...), custom_call_target="tpu_custom_call" | custom-call | flops 1000000 | bytes 1048576 | tf_op jit(solution)/shard_map/pallas_call | solution.py:55
  (20 shorter events, 0.2 us)
Async XLA Ops:
  1.8 11.6 %collective-permute-start = (bf16[64,512]{1,0:T(8,128)(2,1)S(1)}, bf16[64,512]{1,0:T(8,128)(2,1)S(1)}, u32[]{:S(2)}, u32[]{:S(2)}) collective-permute-start(bf16[64,512]{1,0:T(8,128)(2,1)S(1)} %get-tuple-element.61), channel_id=1, source_target_pairs={{0,30},{2,4},{4,2},{6,8},{8,6},{10,12},{12,10},{14,16},{16,14},{18... | collective-permute-start | bytes 196616 | tf_op jit(solution)/shard_map/ppermute | solution.py:382
  8.9 4.6 %collective-permute-start.1 = (bf16[64,512]{1,0:T(8,128)(2,1)S(1)}, bf16[64,512]{1,0:T(8,128)(2,1)S(1)}, u32[]{:S(2)}, u32[]{:S(2)}) collective-permute-start(bf16[64,512]{1,0:T(8,128)(2,1)S(1)} %get-tuple-element.62), channel_id=1, source_target_pairs={{0,2},{2,0},{4,6},{6,4},{8,10},{10,8},{12,14},{14,12},{16,18},{18,... | collective-permute-start | bytes 196616 | tf_op jit(solution)/shard_map/ppermute | solution.py:382
  8.9 4.6 %collective-permute-start.2 = (bf16[64,512]{1,0:T(8,128)(2,1)S(1)}, bf16[64,512]{1,0:T(8,128)(2,1)S(1)}, u32[]{:S(2)}, u32[]{:S(2)}) collective-permute-start(bf16[64,512]{1,0:T(8,128)(2,1)S(1)} %get-tuple-element.63), channel_id=1, source_target_pairs={{0,1},{1,0},{2,3},{3,2},{4,5},{5,4},{6,7},{7,6},{8,9},{9,8},{10,11... | collective-permute-start | bytes 196616 | tf_op jit(solution)/shard_map/ppermute | solution.py:382
  16.9 2.4 %collective-permute-start.3 = (bf16[16,128,128]{2,1,0:T(8,128)(2,1)S(1)}, bf16[16,128,128]{2,1,0:T(8,128)(2,1)S(1)}, u32[]{:S(2)}, u32[]{:S(2)}) collective-permute-start(bf16[16,128,128]{2,1,0:T(8,128)(2,1)S(1)} %shard_map.143), channel_id=1, source_target_pairs={{0,1},{1,0},{2,3},{3,2},{4,5},{5,4},{6,7},{7,6},{8,9},{9,8},{10,11... | collective-permute-start | bytes 1572872 | tf_op jit(solution)/shard_map/ppermute | solution.py:438
  18.4 4.0 %collective-permute-start.10 = (bf16[16,128,128]{2,1,0:T(8,128)(2,1)S(1)}, bf16[16,128,128]{2,1,0:T(8,128)(2,1)S(1)}, u32[]{:S(2)}, u32[]{:S(2)}) collective-permute-start(bf16[16,128,128]{2,1,0:T(8,128)(2,1)S(1)} %shard_map.149), channel_id=1, source_target_pairs={{0,1},{1,0},{2,3},{3,2},{4,5},{5,4},{6,7},{7,6},{8,9},{9,8},{10,11... | collective-permute-start | bytes 1572872 | tf_op jit(solution)/shard_map/ppermute | solution.py:438
  19.5 6.4 %collective-permute-start.4 = (bf16[8,128,128]{2,1,0:T(8,128)(2,1)S(1)}, bf16[8,128,128]{2,1,0:T(8,128)(2,1)S(1)}, u32[]{:S(2)}, u32[]{:S(2)}) collective-permute-start(bf16[8,128,128]{2,1,0:T(8,128)(2,1)S(1)} %get-tuple-element.72), channel_id=1, source_target_pairs={{0,2},{1,5},{2,0},{3,7},{4,6},{5,1},{6,4},{7,3},{8,10},{9,13},{10,... | collective-permute-start | bytes 786440 | tf_op jit(solution)/shard_map/ppermute | solution.py:343
  22.6 6.9 %collective-permute-start.11 = (bf16[8,128,128]{2,1,0:T(8,128)(2,1)S(1)}, bf16[8,128,128]{2,1,0:T(8,128)(2,1)S(1)}, u32[]{:S(2)}, u32[]{:S(2)}) collective-permute-start(bf16[8,128,128]{2,1,0:T(8,128)(2,1)S(1)} %get-tuple-element.88), channel_id=1, source_target_pairs={{0,2},{1,5},{2,0},{3,7},{4,6},{5,1},{6,4},{7,3},{8,10},{9,13},{10,... | collective-permute-start | bytes 786440 | tf_op jit(solution)/shard_map/ppermute | solution.py:343
  26.0 7.1 %collective-permute-start.5 = (bf16[4,128,128]{2,1,0:T(8,128)(2,1)S(1)}, bf16[4,128,128]{2,1,0:T(8,128)(2,1)S(1)}, u32[]{:S(2)}, u32[]{:S(2)}) collective-permute-start(bf16[4,128,128]{2,1,0:T(8,128)(2,1)S(1)} %get-tuple-element.78), channel_id=1, source_target_pairs={{0,4},{1,3},{2,6},{3,1},{4,0},{5,7},{6,2},{7,5},{8,12},{9,11},{10,... | collective-permute-start | bytes 393224 | tf_op jit(solution)/shard_map/ppermute | solution.py:343
  29.5 5.0 %collective-permute-start.12 = (bf16[4,128,128]{2,1,0:T(8,128)(2,1)S(1)}, bf16[4,128,128]{2,1,0:T(8,128)(2,1)S(1)}, u32[]{:S(2)}, u32[]{:S(2)}) collective-permute-start(bf16[4,128,128]{2,1,0:T(8,128)(2,1)S(1)} %get-tuple-element.90), channel_id=1, source_target_pairs={{0,4},{1,3},{2,6},{3,1},{4,0},{5,7},{6,2},{7,5},{8,12},{9,11},{10,... | collective-permute-start | bytes 393224 | tf_op jit(solution)/shard_map/ppermute | solution.py:343
  29.6 8.4 %collective-permute-start.7 = (bf16[64,512]{1,0:T(8,128)(2,1)S(1)}, bf16[64,512]{1,0:T(8,128)(2,1)S(1)}, u32[]{:S(2)}, u32[]{:S(2)}) collective-permute-start(bf16[64,512]{1,0:T(8,128)(2,1)S(1)} %get-tuple-element.80), channel_id=1, source_target_pairs={{30,0},{4,2},{2,4},{8,6},{6,8},{12,10},{10,12},{16,14},{14,16},{20... | collective-permute-start | bytes 196616 | tf_op jit(solution)/shard_map/ppermute | solution.py:471
  33.1 4.9 %collective-permute-start.8 = (bf16[64,512]{1,0:T(8,128)(2,1)S(1)}, bf16[64,512]{1,0:T(8,128)(2,1)S(1)}, u32[]{:S(2)}, u32[]{:S(2)}) collective-permute-start(bf16[64,512]{1,0:T(8,128)(2,1)S(1)} %get-tuple-element.81), channel_id=1, source_target_pairs={{2,0},{0,2},{6,4},{4,6},{10,8},{8,10},{14,12},{12,14},{18,16},{16,... | collective-permute-start | bytes 196616 | tf_op jit(solution)/shard_map/ppermute | solution.py:471
  33.1 4.9 %collective-permute-start.9 = (bf16[64,512]{1,0:T(8,128)(2,1)S(1)}, bf16[64,512]{1,0:T(8,128)(2,1)S(1)}, u32[]{:S(2)}, u32[]{:S(2)}) collective-permute-start(bf16[64,512]{1,0:T(8,128)(2,1)S(1)} %get-tuple-element.82), channel_id=1, source_target_pairs={{1,0},{0,1},{3,2},{2,3},{5,4},{4,5},{7,6},{6,7},{9,8},{8,9},{11,10... | collective-permute-start | bytes 196616 | tf_op jit(solution)/shard_map/ppermute | solution.py:471
  33.1 5.0 %collective-permute-start.6 = (bf16[2,128,128]{2,1,0:T(8,128)(2,1)S(1)}, bf16[2,128,128]{2,1,0:T(8,128)(2,1)S(1)}, u32[]{:S(2)}, u32[]{:S(2)}) collective-permute-start(bf16[2,128,128]{2,1,0:T(8,128)(2,1)S(1)} %get-tuple-element.79), channel_id=1, source_target_pairs={{0,8},{1,9},{2,10},{3,11},{4,12},{5,13},{6,14},{7,15},{8,0},{9,1},... | collective-permute-start | bytes 196616 | tf_op jit(solution)/shard_map/ppermute | solution.py:343
  34.6 4.7 %collective-permute-start.13 = (bf16[2,128,128]{2,1,0:T(8,128)(2,1)S(1)}, bf16[2,128,128]{2,1,0:T(8,128)(2,1)S(1)}, u32[]{:S(2)}, u32[]{:S(2)}) collective-permute-start(bf16[2,128,128]{2,1,0:T(8,128)(2,1)S(1)} %get-tuple-element.92), channel_id=1, source_target_pairs={{0,8},{1,9},{2,10},{3,11},{4,12},{5,13},{6,14},{7,15},{8,0},{9,1},... | collective-permute-start | bytes 196616 | tf_op jit(solution)/shard_map/ppermute | solution.py:343
  39.3 8.0 %collective-permute-start.14 = (bf16[2,128,128]{2,1,0:T(8,128)(2,1)S(1)}, bf16[2,128,128]{2,1,0:T(8,128)(2,1)S(1)}, u32[]{:S(2)}, u32[]{:S(2)}) collective-permute-start(bf16[2,128,128]{2,1,0:T(8,128)(2,1)S(1)} %get-tuple-element.97), channel_id=1, source_target_pairs={{0,16},{1,17},{2,18},{3,19},{4,20},{5,21},{6,22},{7,23},{8,24},{9,... | collective-permute-start | bytes 196616 | tf_op jit(solution)/shard_map/ppermute | solution.py:343
  39.5 8.8 %collective-permute-start.15 = (bf16[2,128,128]{2,1,0:T(8,128)(2,1)S(1)}, bf16[2,128,128]{2,1,0:T(8,128)(2,1)S(1)}, u32[]{:S(2)}, u32[]{:S(2)}) collective-permute-start(bf16[2,128,128]{2,1,0:T(8,128)(2,1)S(1)} %get-tuple-element.98), channel_id=1, source_target_pairs={{0,16},{1,17},{2,18},{3,19},{4,20},{5,21},{6,22},{7,23},{8,24},{9,... | collective-permute-start | bytes 196616 | tf_op jit(solution)/shard_map/ppermute | solution.py:343
  48.4 12.1 %collective-permute-start.16 = (f32[2,128,256]{2,1,0:T(8,128)S(1)}, f32[2,128,256]{2,1,0:T(8,128)S(1)}, u32[]{:S(2)}, u32[]{:S(2)}) collective-permute-start(f32[2,128,256]{2,1,0:T(8,128)S(1)} %get-tuple-element.99.own_ref), channel_id=1, source_target_pairs={{0,1},{1,0},{2,3},{3,2},{4,5},{5,4},{6,7},{7,6},{8,9},{9,8},{10,11... | collective-permute-start | bytes 786440 | tf_op jit(solution)/shard_map/ppermute | solution.py:504
  48.5 3.7 %collective-permute-start.17 = (f32[2,256]{1,0:T(2,128)S(1)}, f32[2,256]{1,0:T(2,128)S(1)}, u32[]{:S(2)}, u32[]{:S(2)}) collective-permute-start(f32[2,256]{1,0:T(2,128)S(1)} %get-tuple-element.100), channel_id=1, source_target_pairs={{0,2},{2,0},{4,6},{6,4},{8,10},{10,8},{12,14},{14,12},{16,18},{18,... | collective-permute-start | bytes 6152 | tf_op jit(solution)/shard_map/ppermute | solution.py:506
  52.1 3.6 %collective-permute-start.18 = (f32[2,256]{1,0:T(2,128)S(1)}, f32[2,256]{1,0:T(2,128)S(1)}, u32[]{:S(2)}, u32[]{:S(2)}) collective-permute-start(f32[2,256]{1,0:T(2,128)S(1)} %add.9), channel_id=1, source_target_pairs={{0,4},{2,6},{4,0},{6,2},{8,12},{10,14},{12,8},{14,10},{16,20},{18,... | collective-permute-start | bytes 6152 | tf_op jit(solution)/shard_map/ppermute | solution.py:506
  55.7 3.6 %collective-permute-start.19 = (f32[2,256]{1,0:T(2,128)S(1)}, f32[2,256]{1,0:T(2,128)S(1)}, u32[]{:S(2)}, u32[]{:S(2)}) collective-permute-start(f32[2,256]{1,0:T(2,128)S(1)} %add.10), channel_id=1, source_target_pairs={{0,8},{2,10},{4,12},{6,14},{8,0},{10,2},{12,4},{14,6},{16,24},{18,... | collective-permute-start | bytes 6152 | tf_op jit(solution)/shard_map/ppermute | solution.py:506
  59.3 1.2 %collective-permute-start.20 = (f32[2,256]{1,0:T(2,128)S(1)}, f32[2,256]{1,0:T(2,128)S(1)}, u32[]{:S(2)}, u32[]{:S(2)}) collective-permute-start(f32[2,256]{1,0:T(2,128)S(1)} %add.11.sums_ref), channel_id=1, source_target_pairs={{0,1},{1,0},{2,3},{3,2},{4,5},{5,4},{6,7},{7,6},{8,9},{9,8},{10,11... | collective-permute-start | bytes 6152 | tf_op jit(solution)/shard_map/ppermute | solution.py:507

commit v3 on v2

--- a/solution.py
+++ b/solution.py
@@ -7,6 +7,7 @@
 from jax.experimental import pallas as pl
 from jax.experimental.pallas import tpu as pltpu
 from jax.sharding import PartitionSpec as P
+
 
 BF = jnp.bfloat16
 F32 = jnp.float32
@@ -76,6 +77,7 @@
 
 
 CHAINS = 2
+TILES = 1
 VMEM_LIMIT = 24 * 1024 * 1024
 
 
@@ -112,6 +114,8 @@
     cot_ref,
     w_first_ref,
     w_second_ref,
+    w_second_t_ref,
+    sender_rows_ref,
     sender_ref,
     receiver_ref,
     edge_ref,
@@ -135,7 +139,9 @@
         row = jnp.where(here, sender - begin + (nodes + k * slots), row)
     table_rows = sender_hot_ref.shape[0]
     ids = lax.broadcasted_iota(jnp.int32, (table_rows, edges), 0)
-    sender_hot_ref[...] = jnp.where(ids == row, 1.0, 0.0).astype(BF)
+    sender_hot = jnp.where(ids == row, 1.0, 0.0).astype(BF)
+    sender_hot_ref[...] = sender_hot
+    sender_rows_ref[...] = sender_hot.T
     copies[1].wait()
     ids = lax.broadcasted_iota(jnp.int32, (nodes, edges), 0)
     receiver_hot = jnp.where(ids == receiver_ref[...], 1.0, 0.0).astype(BF)
@@ -154,6 +160,7 @@
     first = w_first_ref[...].astype(F32)
     weight_sq_ref[0:1, :] = jnp.sum(first * first, 0, keepdims=True)
     copies[5].wait()
+    w_second_t_ref[...] = w_second_ref[...].T
     second = w_second_ref[...].astype(F32)
     weight_sq_ref[1:2, :] = jnp.sum(second * second, 0, keepdims=True)
 
@@ -161,21 +168,22 @@
 def middle_body(*refs, blocks, tile):
     (
         start_ref,
-        sender_hot_ref,
+        sender_rows_ref,
         up_ref,
         node_ref,
         w_first_ref,
         w_second_ref,
+        w_second_t_ref,
         vectors_ref,
-    ) = refs[:7]
-    received = refs[7 : 7 + blocks]
-    pre_back_ref, norm_back_ref, act_t_ref = refs[7 + blocks :]
+    ) = refs[:8]
+    received = refs[8 : 8 + blocks]
+    pre_back_ref, norm_back_ref, act_t_ref = refs[8 + blocks :]
     width = node_ref.shape[1]
     table = jnp.concatenate([node_ref[...]] + [r[...] for r in received], 0)
     bias, gain = vectors_ref[1:2], vectors_ref[2:3]
     for begin in range(0, start_ref.shape[0], tile):
         part = slice(begin, begin + tile)
-        rows = mm(sender_hot_ref[:, part], table, INNER).astype(BF)
+        rows = mm(sender_rows_ref[part], table).astype(BF)
         preact = start_ref[part] + mm(rows, w_first_ref[width : 2 * width])
         sigma = 1.0 / (1.0 + jnp.exp(-preact))
         activation = (preact * sigma).astype(BF)
@@ -195,7 +203,7 @@
             )
         ).astype(BF)
         norm_back_ref[part] = norm_back
-        back = mm(norm_back, w_second_ref[...], OUTER)
+        back = mm(norm_back, w_second_t_ref[...])
         pre_back_ref[part] = (back * (sigma * (1.0 + preact * (1.0 - sigma)))).astype(BF)
 
 
@@ -204,15 +212,15 @@
     return (lax.axis_index("narrow") // (narrow // 2)) % 2
 
 
-def outer_body(*refs, blocks, own, chain):
+def outer_body(*refs, blocks, own):
     (edge_t_ref, act_t_ref, sender_hot_ref, receiver_hot_ref, pre_back_ref, norm_back_ref) = refs[:6]
     node_ref = refs[6]
     received = refs[7 : 7 + blocks]
-    out_ref = refs[7 + blocks]
-    span = out_ref.shape[2]
+    out_refs = refs[7 + blocks :]
+    wide, _, span = out_refs[0].shape
+    width = CHAINS * span
     half = half_bit() if own else 1 - half_bit()
-    begin = pl.multiple_of(half * (CHAINS * span) + chain * span, span)
-    columns = pl.ds(begin, span)
+    columns = pl.ds(pl.multiple_of(half * width, width), width)
     pre_back = pre_back_ref[:, columns]
     node = node_ref[...]
     table = jnp.concatenate([node] + [r[...] for r in received], 0)
@@ -229,14 +237,15 @@
         0,
     )
     second = mm(act_t_ref[...], norm_back_ref[:, columns])
-    wide = out_ref.shape[0]
     first_rows = first.shape[0] // wide
     second_rows = second.shape[0] // wide
-    for w in range(wide):
-        out_ref[w, :first_rows] = first[w * first_rows : (w + 1) * first_rows].astype(out_ref.dtype)
-        out_ref[w, first_rows:] = second[w * second_rows : (w + 1) * second_rows].astype(
-            out_ref.dtype
-        )
+    for c, out_ref in enumerate(out_refs):
+        part = slice(c * span, (c + 1) * span)
+        for w in range(wide):
+            block = first[w * first_rows : (w + 1) * first_rows, part]
+            out_ref[w, :first_rows] = block.astype(out_ref.dtype)
+            block = second[w * second_rows : (w + 1) * second_rows, part]
+            out_ref[w, first_rows:] = block.astype(out_ref.dtype)
 
 
 def back_body(*refs, blocks, slots):
@@ -343,7 +352,7 @@
     return lax.ppermute(value, ("wide", "narrow"), pairs)
 
 
-def per_device(
+def device_step(
     node_latent,
     edge_latent,
     node_cotangent,
@@ -382,7 +391,7 @@
         lax.ppermute(block, axis, pairs) for block, (axis, (pairs, _, _)) in zip(outgoing, routes)
     ]
     vectors = jnp.stack([v.astype(F32) for v in (bias_first, bias_second, norm_gain)], 0)
-    start, sender_hot, receiver_hot, edge_t, up, weight_sq, cot, weights, weights_2 = local_call(
+    start, sender_hot, receiver_hot, edge_t, up, weight_sq, cot, weights, weights_2, weights_2t, sender_rows = local_call(
         functools.partial(prepare_body, slots=slots),
         [
             like((edges, width), F32),
@@ -394,6 +403,8 @@
             like((nodes, width), BF),
             like(w_first.shape, BF),
             like(w_second.shape, BF),
+            like(w_second.shape[::-1], BF),
+            like((edges, table_rows), BF),
         ],
         (
             edge_sender.reshape(1, edges),
@@ -415,9 +426,9 @@
         ],
     )
     pre_back, norm_back, act_t = local_call(
-        functools.partial(middle_body, blocks=blocks, tile=edges // 2),
+        functools.partial(middle_body, blocks=blocks, tile=edges // TILES),
         [like((edges, width), BF), like((edges, width), BF), like((width, edges), BF)],
-        (start, sender_hot, up, node, weights, weights_2, vectors, *received),
+        (start, sender_rows, up, node, weights, weights_2, weights_2t, vectors, *received),
         1.0,
     )
     first_rows, second_rows = w_first.shape[0] // wide, w_second.shape[0] // wide
@@ -425,18 +436,17 @@
     span = width // 2 // CHAINS
     operands = (edge_t, act_t, sender_hot, receiver_hot, pre_back, norm_back, node, *received)
 
-    def outer(own, chain, kind):
-        (grad,) = local_call(
-            functools.partial(outer_body, blocks=blocks, own=own, chain=chain),
-            [like((wide, rows, span), kind)],
+    def outer(own, kind):
+        return local_call(
+            functools.partial(outer_body, blocks=blocks, own=own),
+            [like((wide, rows, span), kind)] * CHAINS,
             operands,
-            0.6 / CHAINS,
+            0.6,
         )
-        return grad
 
     half_swap = swap_pairs(narrow, narrow // 2)
-    gots = [lax.ppermute(outer(False, c, BF), "narrow", half_swap) for c in range(CHAINS)]
-    kepts = [outer(True, c, F32) for c in range(CHAINS)]
+    gots = [lax.ppermute(sent, "narrow", half_swap) for sent in outer(False, BF)]
+    kepts = list(outer(True, F32))
     edge_grad, own_grad, *halo_grad = local_call(
         functools.partial(back_body, blocks=blocks, slots=slots),
         [like((edges, width), BF), like((nodes, width), F32), *halo],
@@ -465,17 +475,6 @@
                 0.01,
             )
             gots[c] = crossed(sent, *masks)
-        if step == 0:
-            gots[-1], halo_grad = lax.optimization_barrier((gots[-1], halo_grad))
-            returned = [
-                lax.ppermute(block, axis, [(t, s) for s, t in pairs])
-                for block, (axis, (pairs, _, _)) in zip(halo_grad, routes)
-            ]
-        if step == bits - 2:
-            gots[-1], returned = lax.optimization_barrier((gots[-1], returned))
-    (node_grad,) = local_call(
-        return_body, [like((nodes, width), BF)], (send_slots, own_grad, *returned), 0.1
-    )
     top = wide // 2
     shape = (2, rows, span)
     for c in range(CHAINS):
@@ -495,6 +494,12 @@
                 )
                 mask *= 2
             kepts[c], gots[c] = value, jnp.zeros(value.shape, BF)
+    returned = []
+    for block, (axis, (pairs, _, _)) in zip(halo_grad, routes):
+        returned.append(lax.ppermute(block, axis, [(t, s) for s, t in pairs]))
+    (node_grad,) = local_call(
+        return_body, [like((nodes, width), BF)], (send_slots, own_grad, *returned), 0.1
+    )
     value, sums = local_call(
         functools.partial(sums_body, first_rows=first_rows),
         [like((2, rows, width // 2), F32), like((2, width // 2), F32)],
@@ -503,7 +508,8 @@
     )
     other = lax.ppermute(value, "narrow", half_swap)
     for position in range(bits - 1):
-        sums = sums + lax.ppermute(sums, "wide", swap_pairs(wide, 1 << position))
+        arrived = lax.ppermute(sums, "wide", swap_pairs(wide, 1 << position))
+        sums = sums + arrived
     other_sums = lax.ppermute(sums, "narrow", half_swap)
     first_update, second_update = local_call(
         functools.partial(clip_body, top=top),
@@ -516,7 +522,7 @@
 
 def solution(mesh):
     return jax.shard_map(
-        per_device,
+        device_step,
         mesh=mesh,
         in_specs=(
             P(("wide", "narrow"), None),

time: 61.5 us -> 62.8 us (1.021)
  waiting for transfers between devices: 24.2 us -> 28.9 us
  Pallas kernels: 14.3 us -> 12.3 us
  starting transfers between devices: 19.9 us -> 18.6 us
    ppermute x8, waiting for transfers between devices: 11.7 us -> 20.6 us  [crossed(): return lax.ppermute(value, ('wide', 'narrow'), pairs)]
    ppermute x13, waiting for transfers between devices: 12.5 us -> 8.27 us  [the longest x3 7.57 us: device_step(): arrived = lax.ppermute(sums, 'wide', swap_pairs(wide, 1 << position))]
    ppermute x8, starting transfers between devices: 7.39 us -> 3.87 us  [crossed(): return lax.ppermute(value, ('wide', 'narrow'), pairs)]
    ppermute x13, starting transfers between devices: 12.5 us -> 14.7 us  [the longest x3 7.03 us: device_step(): lax.ppermute(block, axis, pairs)]
    pallas_call x19 -> x17, Pallas kernels: 14.3 us -> 12.3 us  [local_call(): pl.pallas_call(body, out_shape=outs, in_specs=[hbm] * far + [vmem] * (len...]
  transfers between devices with their start and end apart: 21 -> 21, of which waited for: 12 -> 13; matrix products, arithmetic and copies ran while one was open for 3% -> 3% of each run, Pallas kernels for 14% -> 12%
where the time goes in v3:
time: 62.8 us; the launch traced here: 62.6 us
  waiting for transfers between devices  28.9 us (46%)
  starting transfers between devices  18.6 us (30%)
  Pallas kernels  12.3 us (20%)
  local copies, waits for them, and re-layouts  2.05 us (3%)
  between operations  0.79 us (1%)
    ppermute x8, waiting for transfers between devices, crossed(): return lax.ppermute(value, ('wide', 'narrow'), pairs)  20.6 us
    pallas_call x17, Pallas kernels, local_call(): pl.pallas_call(body, out_shape=outs, in_specs=[hbm] * far + [vmem] * (len...  12.3 us
    ppermute x3, waiting for transfers between devices, device_step(): arrived = lax.ppermute(sums, 'wide', swap_pairs(wide, 1 << position))  7.57 us
    ppermute x3, starting transfers between devices, device_step(): lax.ppermute(block, axis, pairs)  7.03 us
    ppermute x8, starting transfers between devices, crossed(): return lax.ppermute(value, ('wide', 'narrow'), pairs)  3.87 us
    ppermute x3, starting transfers between devices, device_step(): arrived = lax.ppermute(sums, 'wide', swap_pairs(wide, 1 << position))  3.68 us
    ppermute x3, starting transfers between devices, device_step(): returned.append(lax.ppermute(block, axis, [(t, s) for s, t in pairs]))  3.26 us
    another operation x3, local copies, waits for them, and re-layouts, device_step(): jnp.stack([v.astype(F32) for v in (bias_first, bias_second, norm_gain)], 0)  2.05 us
  transfers between devices with their start and end apart: 21, of which 13 were waited for; matrix products, arithmetic and copies ran while one was open for 3% of the time, Pallas kernels for 12%

profile of v3, /device:TPU:0, one launch (start us, length us, event | category | flops | bytes accessed | tf_op | source)
XLA Modules:
  0.0 62.6 jit_solution(5361112334422753628)
XLA Ops:
  0.6 1.2 %shard_map.138 = (s32[1,4,64]{2,1,0:T(4,128)S(1)}, bf16[128,512]{1,0:T(8,128)(2,1)S(1)}, bf16[64,512]{1,0:T(8,128)(2,1)S(1)}, bf16[64,512]{1,0:T(8,128)(2,1)S(1)}, bf16[64,512]{1,0:T(8,128)(2,1)S(1)}) custom-call(s32[1,4,64]{2,1,0:T(4,128)} %send_hbm.1, bf16[128,512]{1,0:T(8,128)(2,1)} %node_hbm.1), custom_call_target="tpu_custom_call" | custom-call | flops 100000000 | bytes 1048576 | tf_op jit(solution)/shard_map/pallas_call | solution.py:56
  1.8 7.0 %collective-permute-start = (bf16[64,512]{1,0:T(8,128)(2,1)S(1)}, bf16[64,512]{1,0:T(8,128)(2,1)S(1)}, u32[]{:S(2)}, u32[]{:S(2)}) collective-permute-start(bf16[64,512]{1,0:T(8,128)(2,1)S(1)} %get-tuple-element.60), channel_id=1, source_target_pairs={{0,30},{2,4},{4,2},{6,8},{8,6},{10,12},{12,10},{14,16},{16,14},{18... | collective-permute-start | bytes 196616 | tf_op jit(solution)/shard_map/ppermute | solution.py:391
  8.9 0.7 %stack.17 = bf16[1,512]{1,0:T(2,128)(2,1)S(1)} reshape(bf16[512]{0:T(512)(128)(2,1)} %param.15) | data formatting | bytes 2048 | tf_op jit(solution)/shard_map/stack | solution.py:393
  9.5 0.7 %stack.18 = bf16[1,512]{1,0:T(2,128)(2,1)S(1)} reshape(bf16[512]{0:T(512)(128)(2,1)} %param.17) | data formatting | bytes 2048 | tf_op jit(solution)/shard_map/stack | solution.py:393
  10.2 0.7 %stack.19 = bf16[1,512]{1,0:T(2,128)(2,1)S(1)} reshape(bf16[512]{0:T(512)(128)(2,1)} %param.18) | data formatting | bytes 2048 | tf_op jit(solution)/shard_map/stack | solution.py:393
  10.9 2.6 %shard_map.139 = (f32[512,512]{1,0:T(8,128)S(1)}, bf16[320,512]{1,0:T(8,128)(2,1)S(1)}, bf16[128,512]{1,0:T(8,128)(2,1)S(1)}, bf16[512,512]{1,0:T(8,128)(2,1)S(1...) custom-call(s32[1,512]{1,0:T(1,128)} %bitcast.2, ...), custom_call_target="tpu_custom_call" | custom-call | flops 1000000000 | bytes 1048576 | tf_op jit(solution)/shard_map/pallas_call | solution.py:56
  13.6 0.0 collective-permute-done.refs_8_.refs_7_
  13.6 0.0 collective-permute-done.1.refs_9_.refs_8_
  13.6 1.9 %shard_map.140 = (bf16[512,512]{1,0:T(8,128)(2,1)S(1)}, bf16[512,512]{1,0:T(8,128)(2,1)S(1)}, bf16[512,512]{1,0:T(8,128)(2,1)S(1)}) custom-call(f32[512,512]{1,0:T(8,128)S(1)} %get-tuple-element.54.refs_0_, bf16[512,320]{1,0:T(8,128)(2,1)S(1)} %get-tuple-element.55.refs_1_, bf16[512,512]{1,0:T(8,128)(2,1)S(1)} %get-tuple-element.56.refs_2_, ...), custom_call_target="tpu_custom_call" | custom-call | flops 1000000000 | bytes 1048576 | tf_op jit(solution)/shard_map/pallas_call | solution.py:56
  15.5 1.0 %shard_map.144 = (bf16[16,128,128]{2,1,0:T(8,128)(2,1)S(1)}, bf16[16,128,128]{2,1,0:T(8,128)(2,1)S(1)}) custom-call(bf16[512,512]{1,0:T(8,128)(2,1)S(1)} %get-tuple-element.72.refs_0_, bf16[512,512]{1,0:T(8,128)(2,1)S(1)} %get-tuple-element.73.refs_1_, bf16[320,512]{1,0:T(8,128)(2,1)S(1)} %get-tuple-element.65.refs_4_.refs_2_, ...), custom_call_target="tpu_custom_call" | custom-call | flops 600000000 | bytes 1048576 | tf_op jit(solution)/shard_map/pallas_call | solution.py:56
  16.6 0.6 collective-permute-start.6
  17.1 0.1 collective-permute-start.10
  17.2 1.0 %shard_map.143 = (f32[16,128,128]{2,1,0:T(8,128)S(1)}, f32[16,128,128]{2,1,0:T(8,128)S(1)}) custom-call(bf16[512,512]{1,0:T(8,128)(2,1)S(1)} %get-tuple-element.72.refs_0_, bf16[512,512]{1,0:T(8,128)(2,1)S(1)} %get-tuple-element.73.refs_1_, bf16[320,512]{1,0:T(8,128)(2,1)S(1)} %get-tuple-element.65.refs_4_.refs_2_, ...), custom_call_target="tpu_custom_call" | custom-call | flops 600000000 | bytes 1048576 | tf_op jit(solution)/shard_map/pallas_call | solution.py:56
  18.2 0.5 collective-permute-done.6.got_ref
  18.7 0.1 shard_map.145
  18.8 2.1 %collective-permute-start.7 = (bf16[8,128,128]{2,1,0:T(8,128)(2,1)S(1)}, bf16[8,128,128]{2,1,0:T(8,128)(2,1)S(1)}, u32[]{:S(2)}, u32[]{:S(2)}) collective-permute-start(bf16[8,128,128]{2,1,0:T(8,128)(2,1)S(1)} %get-tuple-element.78), channel_id=1, source_target_pairs={{0,2},{1,5},{2,0},{3,7},{4,6},{5,1},{6,4},{7,3},{8,10},{9,13},{10,... | collective-permute-start | bytes 786440 | tf_op jit(solution)/shard_map/ppermute | solution.py:352
  20.9 0.1 shard_map.149
  21.0 0.6 collective-permute-start.11
  21.6 3.6 %collective-permute-done.7.got_ref = bf16[8,128,128]{2,1,0:T(8,128)(2,1)S(1)} collective-permute-done((bf16[8,128,128]{2,1,0:T(8,128)(2,1)S(1)}, bf16[8,128,128]{2,1,0:T(8,128)(2,1)S(1)}, u32[]{:S(2)}, u32[]{:S(2)}) %collective-permute-start.7) | collective-permute-done | bytes 262176 | tf_op jit(solution)/shard_map/ppermute | solution.py:352
  25.2 0.1 shard_map.146
  25.3 0.1 collective-permute-start.8
  25.4 2.9 %collective-permute-done.11.got_ref = bf16[8,128,128]{2,1,0:T(8,128)(2,1)S(1)} collective-permute-done((bf16[8,128,128]{2,1,0:T(8,128)(2,1)S(1)}, bf16[8,128,128]{2,1,0:T(8,128)(2,1)S(1)}, u32[]{:S(2)}, u32[]{:S(2)}) %collective-permute-start.11) | collective-permute-done | bytes 262176 | tf_op jit(solution)/shard_map/ppermute | solution.py:352
  28.4 0.1 collective-permute-start.12
  28.4 1.9 %collective-permute-done.8.got_ref = bf16[4,128,128]{2,1,0:T(8,128)(2,1)S(1)} collective-permute-done((bf16[4,128,128]{2,1,0:T(8,128)(2,1)S(1)}, bf16[4,128,128]{2,1,0:T(8,128)(2,1)S(1)}, u32[]{:S(2)}, u32[]{:S(2)}) %collective-permute-start.8) | collective-permute-done | bytes 131104 | tf_op jit(solution)/shard_map/ppermute | solution.py:352
  30.4 0.1 collective-permute-start.9
  30.4 3.0 %collective-permute-done.12.got_ref = bf16[4,128,128]{2,1,0:T(8,128)(2,1)S(1)} collective-permute-done((bf16[4,128,128]{2,1,0:T(8,128)(2,1)S(1)}, bf16[4,128,128]{2,1,0:T(8,128)(2,1)S(1)}, u32[]{:S(2)}, u32[]{:S(2)}) %collective-permute-start.12) | collective-permute-done | bytes 131104 | tf_op jit(solution)/shard_map/ppermute | solution.py:352
  33.4 0.1 collective-permute-start.13
  33.5 1.4 %collective-permute-done.9.got_ref = bf16[2,128,128]{2,1,0:T(8,128)(2,1)S(1)} collective-permute-done((bf16[2,128,128]{2,1,0:T(8,128)(2,1)S(1)}, bf16[2,128,128]{2,1,0:T(8,128)(2,1)S(1)}, u32[]{:S(2)}, u32[]{:S(2)}) %collective-permute-start.9) | collective-permute-done | bytes 65568 | tf_op jit(solution)/shard_map/ppermute | solution.py:352
  35.0 0.6 collective-permute-start.14
  35.5 2.8 %collective-permute-done.13.got_ref = bf16[2,128,128]{2,1,0:T(8,128)(2,1)S(1)} collective-permute-done((bf16[2,128,128]{2,1,0:T(8,128)(2,1)S(1)}, bf16[2,128,128]{2,1,0:T(8,128)(2,1)S(1)}, u32[]{:S(2)}, u32[]{:S(2)}) %collective-permute-start.13) | collective-permute-done | bytes 65568 | tf_op jit(solution)/shard_map/ppermute | solution.py:352
  38.4 0.3 collective-permute-start.15
  38.7 2.4 %collective-permute-done.14.refs_2_ = bf16[2,128,128]{2,1,0:T(8,128)(2,1)S(1)} collective-permute-done((bf16[2,128,128]{2,1,0:T(8,128)(2,1)S(1)}, bf16[2,128,128]{2,1,0:T(8,128)(2,1)S(1)}, u32[]{:S(2)}, u32[]{:S(2)}) %collective-permute-start.14) | collective-permute-done | bytes 65568 | tf_op jit(solution)/shard_map/ppermute | solution.py:352
  41.1 2.5 %collective-permute-done.15.refs_3_ = bf16[2,128,128]{2,1,0:T(8,128)(2,1)S(1)} collective-permute-done((bf16[2,128,128]{2,1,0:T(8,128)(2,1)S(1)}, bf16[2,128,128]{2,1,0:T(8,128)(2,1)S(1)}, u32[]{:S(2)}, u32[]{:S(2)}) %collective-permute-start.15) | collective-permute-done | bytes 65568 | tf_op jit(solution)/shard_map/ppermute | solution.py:352
  43.7 0.1 collective-permute-start.16
  43.8 2.3 %shard_map.141 = (bf16[512,512]{1,0:T(8,128)(2,1)}, f32[128,512]{1,0:T(8,128)S(1)}, bf16[64,512]{1,0:T(8,128)(2,1)S(1)}, bf16[64,512]{1,0:T(8,128)(2,1)S(1)}, bf16[64,512]{1,0:T(8,128)(2,1)S(1)}) custom-call(bf16[512,512]{1,0:T(8,128)(2,1)S(1)} %get-tuple-element.63.refs_0_.refs_4_, bf16[1536,512]{1,0:T(8,128)(2,1)S(1)} %get-tuple-element.57.refs_4_.refs_1_, ...), custom_call_target="tpu_custom_call" | custom-call | flops 1000000000 | bytes 1048576 | tf_op jit(solution)/shard_map/pallas_call | solution.py:56
  46.1 3.1 %collective-permute-start.3 = (bf16[64,512]{1,0:T(8,128)(2,1)S(1)}, bf16[64,512]{1,0:T(8,128)(2,1)S(1)}, u32[]{:S(2)}, u32[]{:S(2)}) collective-permute-start(bf16[64,512]{1,0:T(8,128)(2,1)S(1)} %get-tuple-element.68), channel_id=1, source_target_pairs={{30,0},{4,2},{2,4},{8,6},{6,8},{12,10},{10,12},{16,14},{14,16},{20... | collective-permute-start | bytes 196616 | tf_op jit(solution)/shard_map/ppermute | solution.py:499
  49.1 0.2 collective-permute-start.5
  49.3 1.8 %collective-permute-start.17 = (f32[2,256]{1,0:T(2,128)S(1)}, f32[2,256]{1,0:T(2,128)S(1)}, u32[]{:S(2)}, u32[]{:S(2)}) collective-permute-start(f32[2,256]{1,0:T(2,128)S(1)} %get-tuple-element.96), channel_id=1, source_target_pairs={{0,2},{2,0},{4,6},{6,4},{8,10},{10,8},{12,14},{14,12},{16,18},{18,... | collective-permute-start | bytes 6152 | tf_op jit(solution)/shard_map/ppermute | solution.py:511
  51.2 2.3 %collective-permute-done.17 = f32[2,256]{1,0:T(2,128)S(1)} collective-permute-done((f32[2,256]{1,0:T(2,128)S(1)}, f32[2,256]{1,0:T(2,128)S(1)}, u32[]{:S(2)}, u32[]{:S(2)}) %collective-permute-start.17) | collective-permute-done | bytes 2080 | tf_op jit(solution)/shard_map/ppermute | solution.py:511
  53.4 1.9 %collective-permute-start.18 = (f32[2,256]{1,0:T(2,128)S(1)}, f32[2,256]{1,0:T(2,128)S(1)}, u32[]{:S(2)}, u32[]{:S(2)}) collective-permute-start(f32[2,256]{1,0:T(2,128)S(1)} %add.9), channel_id=1, source_target_pairs={{0,4},{2,6},{4,0},{6,2},{8,12},{10,14},{12,8},{14,10},{16,20},{18,... | collective-permute-start | bytes 6152 | tf_op jit(solution)/shard_map/ppermute | solution.py:511
  55.3 1.7 %collective-permute-done.18 = f32[2,256]{1,0:T(2,128)S(1)} collective-permute-done((f32[2,256]{1,0:T(2,128)S(1)}, f32[2,256]{1,0:T(2,128)S(1)}, u32[]{:S(2)}, u32[]{:S(2)}) %collective-permute-start.18) | collective-permute-done | bytes 2080 | tf_op jit(solution)/shard_map/ppermute | solution.py:511
  57.0 0.0 collective-permute-start.19
  57.0 3.6 %collective-permute-done.19 = f32[2,256]{1,0:T(2,128)S(1)} collective-permute-done((f32[2,256]{1,0:T(2,128)S(1)}, f32[2,256]{1,0:T(2,128)S(1)}, u32[]{:S(2)}, u32[]{:S(2)}) %collective-permute-start.19) | collective-permute-done | bytes 2080 | tf_op jit(solution)/shard_map/ppermute | solution.py:511
  60.6 0.0 collective-permute-start.20
  60.6 0.0 collective-permute-done.3.refs_0_
  60.6 0.9 %shard_map.142 = bf16[128,512]{1,0:T(8,128)(2,1)} custom-call(s32[1,4,64]{2,1,0:T(4,128)S(1)} %get-tuple-element.52.send_ref, f32[128,512]{1,0:T(8,128)S(1)} %get-tuple-element.67.own_ref, bf16[64,512]{1,0:T(8,128)(2,1)S(1)} %collective-permute-done.3.refs_0_, bf16[64,512]{1,0:T(8,128)(2,1)S(1)} %collective-permute-done.4.refs_1_, ...), custom_call_target="tpu_custom_call" | custom-call | flops 100000000 | bytes 1048576 | tf_op jit(solution)/shard_map/pallas_call | solution.py:56
  61.6 0.2 collective-permute-done.20.other_sums_ref
  61.8 0.8 %shard_map.154 = (f32[96,512]{1,0:T(8,128)}, f32[32,512]{1,0:T(8,128)}) custom-call(f32[2,128,256]{2,1,0:T(8,128)S(1)} %get-tuple-element.95.own_ref, f32[2,128,256]{2,1,0:T(8,128)S(1)} %collective-permute-done.16.other_ref, f32[2,256]{1,0:T(2,128)S(1)} %add.11.sums_ref, f32[2,256]{1,0:T(2,128)S(1)} %collective-permute-done.20.other_sums_ref, ...), custom_call_target="tpu_custom_call" | custom-call | flops 1000000 | bytes 1048576 | tf_op jit(solution)/shard_map/pallas_call | solution.py:56
  (18 shorter events, 0.3 us)
Async XLA Ops:
  1.8 11.7 %collective-permute-start = (bf16[64,512]{1,0:T(8,128)(2,1)S(1)}, bf16[64,512]{1,0:T(8,128)(2,1)S(1)}, u32[]{:S(2)}, u32[]{:S(2)}) collective-permute-start(bf16[64,512]{1,0:T(8,128)(2,1)S(1)} %get-tuple-element.60), channel_id=1, source_target_pairs={{0,30},{2,4},{4,2},{6,8},{8,6},{10,12},{12,10},{14,16},{16,14},{18... | collective-permute-start | bytes 196616 | tf_op jit(solution)/shard_map/ppermute | solution.py:391
  8.9 4.7 %collective-permute-start.1 = (bf16[64,512]{1,0:T(8,128)(2,1)S(1)}, bf16[64,512]{1,0:T(8,128)(2,1)S(1)}, u32[]{:S(2)}, u32[]{:S(2)}) collective-permute-start(bf16[64,512]{1,0:T(8,128)(2,1)S(1)} %get-tuple-element.61), channel_id=1, source_target_pairs={{0,2},{2,0},{4,6},{6,4},{8,10},{10,8},{12,14},{14,12},{16,18},{18,... | collective-permute-start | bytes 196616 | tf_op jit(solution)/shard_map/ppermute | solution.py:391
  8.9 4.7 %collective-permute-start.2 = (bf16[64,512]{1,0:T(8,128)(2,1)S(1)}, bf16[64,512]{1,0:T(8,128)(2,1)S(1)}, u32[]{:S(2)}, u32[]{:S(2)}) collective-permute-start(bf16[64,512]{1,0:T(8,128)(2,1)S(1)} %get-tuple-element.62), channel_id=1, source_target_pairs={{0,1},{1,0},{2,3},{3,2},{4,5},{5,4},{6,7},{7,6},{8,9},{9,8},{10,11... | collective-permute-start | bytes 196616 | tf_op jit(solution)/shard_map/ppermute | solution.py:391
  16.6 2.1 %collective-permute-start.6 = (bf16[16,128,128]{2,1,0:T(8,128)(2,1)S(1)}, bf16[16,128,128]{2,1,0:T(8,128)(2,1)S(1)}, u32[]{:S(2)}, u32[]{:S(2)}) collective-permute-start(bf16[16,128,128]{2,1,0:T(8,128)(2,1)S(1)} %get-tuple-element.76), channel_id=1, source_target_pairs={{0,1},{1,0},{2,3},{3,2},{4,5},{5,4},{6,7},{7,6},{8,9},{9,8},{10,11... | collective-permute-start | bytes 1572872 | tf_op jit(solution)/shard_map/ppermute | solution.py:448
  17.1 3.8 %collective-permute-start.10 = (bf16[16,128,128]{2,1,0:T(8,128)(2,1)S(1)}, bf16[16,128,128]{2,1,0:T(8,128)(2,1)S(1)}, u32[]{:S(2)}, u32[]{:S(2)}) collective-permute-start(bf16[16,128,128]{2,1,0:T(8,128)(2,1)S(1)} %get-tuple-element.85), channel_id=1, source_target_pairs={{0,1},{1,0},{2,3},{3,2},{4,5},{5,4},{6,7},{7,6},{8,9},{9,8},{10,11... | collective-permute-start | bytes 1572872 | tf_op jit(solution)/shard_map/ppermute | solution.py:448
  18.8 6.4 %collective-permute-start.7 = (bf16[8,128,128]{2,1,0:T(8,128)(2,1)S(1)}, bf16[8,128,128]{2,1,0:T(8,128)(2,1)S(1)}, u32[]{:S(2)}, u32[]{:S(2)}) collective-permute-start(bf16[8,128,128]{2,1,0:T(8,128)(2,1)S(1)} %get-tuple-element.78), channel_id=1, source_target_pairs={{0,2},{1,5},{2,0},{3,7},{4,6},{5,1},{6,4},{7,3},{8,10},{9,13},{10,... | collective-permute-start | bytes 786440 | tf_op jit(solution)/shard_map/ppermute | solution.py:352
  21.0 7.4 %collective-permute-start.11 = (bf16[8,128,128]{2,1,0:T(8,128)(2,1)S(1)}, bf16[8,128,128]{2,1,0:T(8,128)(2,1)S(1)}, u32[]{:S(2)}, u32[]{:S(2)}) collective-permute-start(bf16[8,128,128]{2,1,0:T(8,128)(2,1)S(1)} %get-tuple-element.87), channel_id=1, source_target_pairs={{0,2},{1,5},{2,0},{3,7},{4,6},{5,1},{6,4},{7,3},{8,10},{9,13},{10,... | collective-permute-start | bytes 786440 | tf_op jit(solution)/shard_map/ppermute | solution.py:352
  25.3 5.0 %collective-permute-start.8 = (bf16[4,128,128]{2,1,0:T(8,128)(2,1)S(1)}, bf16[4,128,128]{2,1,0:T(8,128)(2,1)S(1)}, u32[]{:S(2)}, u32[]{:S(2)}) collective-permute-start(bf16[4,128,128]{2,1,0:T(8,128)(2,1)S(1)} %get-tuple-element.80), channel_id=1, source_target_pairs={{0,4},{1,3},{2,6},{3,1},{4,0},{5,7},{6,2},{7,5},{8,12},{9,11},{10,... | collective-permute-start | bytes 393224 | tf_op jit(solution)/shard_map/ppermute | solution.py:352
  28.4 5.0 %collective-permute-start.12 = (bf16[4,128,128]{2,1,0:T(8,128)(2,1)S(1)}, bf16[4,128,128]{2,1,0:T(8,128)(2,1)S(1)}, u32[]{:S(2)}, u32[]{:S(2)}) collective-permute-start(bf16[4,128,128]{2,1,0:T(8,128)(2,1)S(1)} %get-tuple-element.89), channel_id=1, source_target_pairs={{0,4},{1,3},{2,6},{3,1},{4,0},{5,7},{6,2},{7,5},{8,12},{9,11},{10,... | collective-permute-start | bytes 393224 | tf_op jit(solution)/shard_map/ppermute | solution.py:352
  30.4 4.6 %collective-permute-start.9 = (bf16[2,128,128]{2,1,0:T(8,128)(2,1)S(1)}, bf16[2,128,128]{2,1,0:T(8,128)(2,1)S(1)}, u32[]{:S(2)}, u32[]{:S(2)}) collective-permute-start(bf16[2,128,128]{2,1,0:T(8,128)(2,1)S(1)} %get-tuple-element.82), channel_id=1, source_target_pairs={{0,8},{1,9},{2,10},{3,11},{4,12},{5,13},{6,14},{7,15},{8,0},{9,1},... | collective-permute-start | bytes 196616 | tf_op jit(solution)/shard_map/ppermute | solution.py:352
  33.4 4.9 %collective-permute-start.13 = (bf16[2,128,128]{2,1,0:T(8,128)(2,1)S(1)}, bf16[2,128,128]{2,1,0:T(8,128)(2,1)S(1)}, u32[]{:S(2)}, u32[]{:S(2)}) collective-permute-start(bf16[2,128,128]{2,1,0:T(8,128)(2,1)S(1)} %get-tuple-element.91), channel_id=1, source_target_pairs={{0,8},{1,9},{2,10},{3,11},{4,12},{5,13},{6,14},{7,15},{8,0},{9,1},... | collective-permute-start | bytes 196616 | tf_op jit(solution)/shard_map/ppermute | solution.py:352
  35.0 6.1 %collective-permute-start.14 = (bf16[2,128,128]{2,1,0:T(8,128)(2,1)S(1)}, bf16[2,128,128]{2,1,0:T(8,128)(2,1)S(1)}, u32[]{:S(2)}, u32[]{:S(2)}) collective-permute-start(bf16[2,128,128]{2,1,0:T(8,128)(2,1)S(1)} %get-tuple-element.93), channel_id=1, source_target_pairs={{0,16},{1,17},{2,18},{3,19},{4,20},{5,21},{6,22},{7,23},{8,24},{9,... | collective-permute-start | bytes 196616 | tf_op jit(solution)/shard_map/ppermute | solution.py:352
  38.4 5.2 %collective-permute-start.15 = (bf16[2,128,128]{2,1,0:T(8,128)(2,1)S(1)}, bf16[2,128,128]{2,1,0:T(8,128)(2,1)S(1)}, u32[]{:S(2)}, u32[]{:S(2)}) collective-permute-start(bf16[2,128,128]{2,1,0:T(8,128)(2,1)S(1)} %get-tuple-element.94), channel_id=1, source_target_pairs={{0,16},{1,17},{2,18},{3,19},{4,20},{5,21},{6,22},{7,23},{8,24},{9,... | collective-permute-start | bytes 196616 | tf_op jit(solution)/shard_map/ppermute | solution.py:352
  43.7 18.1 %collective-permute-start.16 = (f32[2,128,256]{2,1,0:T(8,128)S(1)}, f32[2,128,256]{2,1,0:T(8,128)S(1)}, u32[]{:S(2)}, u32[]{:S(2)}) collective-permute-start(f32[2,128,256]{2,1,0:T(8,128)S(1)} %get-tuple-element.95.own_ref), channel_id=1, source_target_pairs={{0,1},{1,0},{2,3},{3,2},{4,5},{5,4},{6,7},{7,6},{8,9},{9,8},{10,11... | collective-permute-start | bytes 786440 | tf_op jit(solution)/shard_map/ppermute | solution.py:509
  46.1 14.5 %collective-permute-start.3 = (bf16[64,512]{1,0:T(8,128)(2,1)S(1)}, bf16[64,512]{1,0:T(8,128)(2,1)S(1)}, u32[]{:S(2)}, u32[]{:S(2)}) collective-permute-start(bf16[64,512]{1,0:T(8,128)(2,1)S(1)} %get-tuple-element.68), channel_id=1, source_target_pairs={{30,0},{4,2},{2,4},{8,6},{6,8},{12,10},{10,12},{16,14},{14,16},{20... | collective-permute-start | bytes 196616 | tf_op jit(solution)/shard_map/ppermute | solution.py:499
  49.1 11.5 %collective-permute-start.4 = (bf16[64,512]{1,0:T(8,128)(2,1)S(1)}, bf16[64,512]{1,0:T(8,128)(2,1)S(1)}, u32[]{:S(2)}, u32[]{:S(2)}) collective-permute-start(bf16[64,512]{1,0:T(8,128)(2,1)S(1)} %get-tuple-element.69), channel_id=1, source_target_pairs={{2,0},{0,2},{6,4},{4,6},{10,8},{8,10},{14,12},{12,14},{18,16},{16,... | collective-permute-start | bytes 196616 | tf_op jit(solution)/shard_map/ppermute | solution.py:499
  49.1 11.5 %collective-permute-start.5 = (bf16[64,512]{1,0:T(8,128)(2,1)S(1)}, bf16[64,512]{1,0:T(8,128)(2,1)S(1)}, u32[]{:S(2)}, u32[]{:S(2)}) collective-permute-start(bf16[64,512]{1,0:T(8,128)(2,1)S(1)} %get-tuple-element.70), channel_id=1, source_target_pairs={{1,0},{0,1},{3,2},{2,3},{5,4},{4,5},{7,6},{6,7},{9,8},{8,9},{11,10... | collective-permute-start | bytes 196616 | tf_op jit(solution)/shard_map/ppermute | solution.py:499
  49.3 4.1 %collective-permute-start.17 = (f32[2,256]{1,0:T(2,128)S(1)}, f32[2,256]{1,0:T(2,128)S(1)}, u32[]{:S(2)}, u32[]{:S(2)}) collective-permute-start(f32[2,256]{1,0:T(2,128)S(1)} %get-tuple-element.96), channel_id=1, source_target_pairs={{0,2},{2,0},{4,6},{6,4},{8,10},{10,8},{12,14},{14,12},{16,18},{18,... | collective-permute-start | bytes 6152 | tf_op jit(solution)/shard_map/ppermute | solution.py:511
  53.4 3.6 %collective-permute-start.18 = (f32[2,256]{1,0:T(2,128)S(1)}, f32[2,256]{1,0:T(2,128)S(1)}, u32[]{:S(2)}, u32[]{:S(2)}) collective-permute-start(f32[2,256]{1,0:T(2,128)S(1)} %add.9), channel_id=1, source_target_pairs={{0,4},{2,6},{4,0},{6,2},{8,12},{10,14},{12,8},{14,10},{16,20},{18,... | collective-permute-start | bytes 6152 | tf_op jit(solution)/shard_map/ppermute | solution.py:511
  57.0 3.6 %collective-permute-start.19 = (f32[2,256]{1,0:T(2,128)S(1)}, f32[2,256]{1,0:T(2,128)S(1)}, u32[]{:S(2)}, u32[]{:S(2)}) collective-permute-start(f32[2,256]{1,0:T(2,128)S(1)} %add.10), channel_id=1, source_target_pairs={{0,8},{2,10},{4,12},{6,14},{8,0},{10,2},{12,4},{14,6},{16,24},{18,... | collective-permute-start | bytes 6152 | tf_op jit(solution)/shard_map/ppermute | solution.py:511
  60.6 1.2 %collective-permute-start.20 = (f32[2,256]{1,0:T(2,128)S(1)}, f32[2,256]{1,0:T(2,128)S(1)}, u32[]{:S(2)}, u32[]{:S(2)}) collective-permute-start(f32[2,256]{1,0:T(2,128)S(1)} %add.11.sums_ref), channel_id=1, source_target_pairs={{0,1},{1,0},{2,3},{3,2},{4,5},{5,4},{6,7},{7,6},{8,9},{9,8},{10,11... | collective-permute-start | bytes 6152 | tf_op jit(solution)/shard_map/ppermute | solution.py:513
